TPU v7x, 32 devices: a whole 2x2x4 slice. The times are simulated.
32 devices in a mesh: ep: 32 (over z, y, x, core).
Axes of the slice: x: 2, y: 2, z: 4, core: 2. Of those that a mesh axis runs over, the one named last changes fastest.
Arguments:
- x_tokens: bfloat16 [262144, 384], P('ep')
- w_router: float32 [384, 32], replicated
- expert_idx: int32 [262144], P('ep')
- w_in: bfloat16 [32, 384, 1536], P('ep')
- w_out: bfloat16 [32, 1536, 384], P('ep')
- grad_y: bfloat16 [262144, 384], P('ep')
Outputs:
- output 1: bfloat16 [262144, 384], P('ep')
- output 2: float32 [32, 384, 1536], P('ep')
- output 3: float32 [32, 1536, 384], P('ep')
- output 4: float32 [384, 32], replicated
- output 5: float32 [], replicated
- output 6: float32 [], replicated
All inputs are finite; a program needn't handle non-finite values.
Results may differ from a plain program's by a relative error of at most 0.0125986.
Values are sent between devices in bfloat16 or wider.
A program may use at most 1 GiB of HBM per device.

v0:
```python
import jax
import jax.numpy as jnp
from jax import lax
from jax.sharding import PartitionSpec as P

AUX_WEIGHT = 0.01
Z_WEIGHT = 0.001


def route_slots(idx_group, num_experts, capacity):
    tokens = idx_group.shape[0]
    n_slots = num_experts * capacity
    onehot = (idx_group[:, None] == jnp.arange(num_experts, dtype=jnp.int32)[None, :]).astype(jnp.int32)
    position = jnp.sum(jnp.cumsum(onehot, axis=0) * onehot, axis=1) - 1
    tok_slot = jnp.where(position < capacity, idx_group * capacity + position, n_slots)
    slot_tok = jnp.full((n_slots,), tokens, jnp.int32).at[tok_slot].set(jnp.arange(tokens, dtype=jnp.int32), mode='drop')
    return onehot.astype(jnp.float32), tok_slot, slot_tok


def gather_rows(source, row_index):
    return jnp.take(source, row_index, axis=0, mode='fill', fill_value=0)


def router_grad(router_prob, onehot, gate_val, d_gate, log_norm, aux_vec, z_coef):
    spread = jnp.sum(router_prob * aux_vec, axis=-1, keepdims=True)
    return ((gate_val * d_gate)[..., None] * (onehot - router_prob)
            + router_prob * (aux_vec - spread)
            + (z_coef * log_norm)[..., None] * router_prob)


def solution(mesh):
    n_dev = mesh.shape['ep']

    def expert_layer(x_tokens, w_router, expert_idx, w_in, w_out, grad_y):
        tokens, d_model = x_tokens.shape
        n_local = w_in.shape[0]
        num_experts = n_local * n_dev
        capacity = (5 * tokens + 4 * num_experts - 1) // (4 * num_experts)
        total_tok = tokens * n_dev
        onehot, tok_slot, slot_tok = route_slots(expert_idx, num_experts, capacity)
        logits = jnp.dot(x_tokens, w_router, preferred_element_type=jnp.float32)
        router_prob = jax.nn.softmax(logits, axis=-1)
        log_norm = jax.nn.logsumexp(logits, axis=-1)
        gate_val = jnp.sum(router_prob * onehot, axis=-1)
        route_stats = jnp.concatenate([jnp.sum(onehot, axis=0), jnp.sum(router_prob, axis=0), jnp.sum(log_norm * log_norm)[None]])
        route_stats = lax.psum(route_stats, 'ep')

        sent_rows = gather_rows(x_tokens, slot_tok).reshape(n_dev, n_local, capacity, d_model)
        recv_rows = lax.all_to_all(sent_rows, 'ep', 0, 0, tiled=True)
        pre_act = jnp.einsum('pecd,edf->pecf', recv_rows, w_in, preferred_element_type=jnp.float32)
        hidden = jnp.maximum(pre_act, 0.0).astype(jnp.bfloat16)
        expert_out = jnp.einsum('pecf,efd->pecd', hidden, w_out, preferred_element_type=jnp.float32).astype(jnp.bfloat16)
        back_out = lax.all_to_all(expert_out, 'ep', 0, 0, tiled=True).reshape(num_experts * capacity, d_model)
        out_tok = gather_rows(back_out, tok_slot)
        gy_f32 = grad_y.astype(jnp.float32)
        d_gate = jnp.sum(out_tok.astype(jnp.float32) * gy_f32, axis=-1)

        scaled = (gate_val[:, None] * gy_f32).astype(jnp.bfloat16)
        sent_grad = gather_rows(scaled, slot_tok).reshape(n_dev, n_local, capacity, d_model)
        recv_grad = lax.all_to_all(sent_grad, 'ep', 0, 0, tiled=True)
        d_hidden = jnp.einsum('pecd,efd->pecf', recv_grad, w_out, preferred_element_type=jnp.float32)
        d_pre = jnp.where(hidden > 0, d_hidden, 0.0).astype(jnp.bfloat16)
        grad_w_out = jnp.einsum('pecf,pecd->efd', hidden, recv_grad, preferred_element_type=jnp.float32)
        grad_w_in = jnp.einsum('pecd,pecf->edf', recv_rows, d_pre, preferred_element_type=jnp.float32)
        d_rows = jnp.einsum('pecf,edf->pecd', d_pre, w_in, preferred_element_type=jnp.float32).astype(jnp.bfloat16)
        back_grad = lax.all_to_all(d_rows, 'ep', 0, 0, tiled=True).reshape(num_experts * capacity, d_model)
        dx_expert = gather_rows(back_grad, tok_slot)

        load_frac = route_stats[:num_experts] / total_tok
        mean_prob = route_stats[num_experts:2 * num_experts] / total_tok
        aux_loss = AUX_WEIGHT * num_experts * jnp.sum(load_frac * mean_prob)
        z_loss = Z_WEIGHT * route_stats[2 * num_experts] / total_tok
        aux_vec = AUX_WEIGHT * num_experts * load_frac / total_tok
        d_logits = router_grad(router_prob, onehot, gate_val, d_gate, log_norm, aux_vec, 2.0 * Z_WEIGHT / total_tok)
        dx_router = jnp.einsum('se,de->sd', d_logits, w_router)
        grad_x = (dx_expert.astype(jnp.float32) + dx_router).astype(jnp.bfloat16)
        grad_w_router = lax.psum(jnp.einsum('sd,se->de', x_tokens, d_logits, preferred_element_type=jnp.float32), 'ep')
        return grad_x, grad_w_in, grad_w_out, grad_w_router, aux_loss, z_loss

    return jax.shard_map(expert_layer, mesh=mesh,
                         in_specs=(P('ep', None), P(None, None), P('ep'), P('ep', None, None), P('ep', None, None), P('ep', None)),
                         out_specs=(P('ep', None), P('ep', None, None), P('ep', None, None), P(None, None), P(), P()),
                         check_vma=False)
```

profile of v0, /device:TPU:0, one launch (start us, length us, event | category | flops | bytes accessed | tf_op | source)
XLA Modules:
  0.0 1153.2 jit_solution(14318799424166788530)
XLA Ops:
  1.6 9.5 reduce-window.6
  14.9 30.5 %scatter_custom_fusion = s32[10240]{0:T(1024)S(1)} fusion(s32[8192]{0:T(1024)S(1)} %get-tuple-element.13, s32[8192]{0:T(1024)S(1)} %iota.11, s32[]{:T(128)} %constant.17.clone.1), kind=kCustom, calls=%fused_computation.65 | custom fusion | bytes 40964 | tf_op jit(solution)/shard_map/scatter | solution.py:16
  45.4 43.9 %gather_fusion = bf16[10240,384]{1,0:T(8,128)(2,1)} fusion(bf16[8192,384]{1,0:T(8,128)(2,1)} %param.10, s32[10240]{0:T(1024)S(1)} %fusion.33), kind=kCustom, calls=%fused_computation.clone | custom fusion | bytes 15769600 | tf_op jit(solution)/shard_map/jit(_take)/gather | solution.py:21
  89.3 5.4 broadcast_select_fusion.1
  94.7 183.5 %all_to_all.20 = bf16[32,1,320,384]{3,2,1,0:T(8,128)(2,1)} all-to-all(bf16[32,1,320,384]{3,2,1,0:T(8,128)(2,1)S(1)} %bitcast.89), channel_id=1, replica_groups=mesh['ep'=32] {'ep'}, dimensions={0} | all-to-all | bytes 15728640 | tf_op jit(solution)/shard_map/all_to_all | solution.py:49
  278.2 30.9 %convert_reduce_fusion = (u32[320,1536]{1,0:T(8,128)}, bf16[32,320,1536]{2,1,0:T(8,128)(2,1)}) fusion(bf16[1,384,1536]{2,1,0:T(8,128)(2,1)S(1)} %copy-done, bf16[32,1,320,384]{3,2,1,0:T(8,128)(2,1)} %all_to_all.20), kind=kOutput, calls=%fused_computation.6 | convolution fusion | flops 12204933120 | bytes 42467328 | tf_op jit(solution)/shard_map/pecd,edf->pecf/dot_general | solution.py:50
  309.1 25.0 %convert_bitcast_fusion = bf16[32,1,320,384]{3,2,1,0:T(8,128)(2,1)} fusion(bf16[32,320,1536]{2,1,0:T(8,128)(2,1)} %get-tuple-element.21, bf16[1,1536,384]{2,1,0:T(8,128)(2,1)} %param.14), kind=kOutput, calls=%fused_computation.20 | convolution fusion | flops 12083527680 | bytes 40501248 | tf_op jit(solution)/shard_map/pecf,efd->pecd/dot_general | solution.py:52
  334.1 7.2 all-to-all-start.3
  341.3 4.8 fusion.39
  348.3 186.2 %psum.14 = f32[65]{0:T(128)S(1)} all-reduce(f32[65]{0:T(128)S(1)} %pad_maximum_fusion), channel_id=1, replica_groups=mesh['ep'=32] {'ep'}, use_global_device_ids=true, to_apply=%region_12.15 | all-reduce | flops 65 | bytes 520 | tf_op jit(solution)/shard_map/psum | solution.py:46
  535.7 36.8 %gather_fusion.3 = bf16[8192,384]{1,0:T(8,128)(2,1)} fusion(bf16[10240,384]{1,0:T(8,128)(2,1)} %bitcast.21, s32[8192]{0:T(1024)S(1)} %broadcast_clamp_fusion), kind=kCustom, calls=%fused_computation.3.clone | custom fusion | bytes 12615680 | tf_op jit(solution)/shard_map/jit(_take)/gather | solution.py:21
  572.5 10.2 fusion.1
  582.7 43.9 %gather_fusion.1 = bf16[10240,384]{1,0:T(8,128)(2,1)} fusion(bf16[8192,384]{1,0:T(8,128)(2,1)} %get-tuple-element.15, s32[10240]{0:T(1024)S(1)} %fusion.33), kind=kCustom, calls=%fused_computation.2.clone | custom fusion | bytes 15769600 | tf_op jit(solution)/shard_map/jit(_take)/gather | solution.py:21
  626.7 5.4 broadcast_select_fusion
  632.0 180.5 %all_to_all.21 = bf16[32,1,320,384]{3,2,1,0:T(8,128)(2,1)} all-to-all(bf16[32,1,320,384]{3,2,1,0:T(8,128)(2,1)S(1)} %bitcast.88), channel_id=1, replica_groups=mesh['ep'=32] {'ep'}, dimensions={0} | all-to-all | bytes 15728640 | tf_op jit(solution)/shard_map/all_to_all | solution.py:60
  812.5 26.8 %select_convert_fusion = bf16[32,320,1536]{2,1,0:T(8,128)(2,1)} fusion(u32[320,1536]{1,0:T(8,128)} %get-tuple-element.20, bf16[32,1,320,384]{3,2,1,0:T(8,128)(2,1)} %all_to_all.21, bf16[1,1536,384]{2,1,0:T(8,128)(2,1)} %param.14), kind=kOutput, calls=%fused_computation.7 | convolution fusion | flops 12158238720 | bytes 42467328 | tf_op jit(solution)/shard_map/pecd,efd->pecf/dot_general | solution.py:61
  839.3 24.5 %convert_bitcast_fusion.1 = bf16[32,1,320,384]{3,2,1,0:T(8,128)(2,1)} fusion(bf16[32,320,1536]{2,1,0:T(8,128)(2,1)} %select_convert_fusion, bf16[1,384,1536]{2,1,0:T(8,128)(2,1)S(1)} %copy-done), kind=kOutput, calls=%fused_computation.21 | convolution fusion | flops 12083527680 | bytes 40501248 | tf_op jit(solution)/shard_map/pecf,edf->pecd/dot_general | solution.py:65
  863.8 3.7 all-to-all-start.2
  869.4 3.9 convolution_bitcast_fusion
  873.2 187.6 %psum.15 = f32[384,32]{0,1:T(8,128)} all-reduce(f32[384,32]{0,1:T(8,128)S(1)} %convolution_bitcast_fusion), channel_id=1, replica_groups=mesh['ep'=32] {'ep'}, use_global_device_ids=true, to_apply=%region_14.17 | all-reduce | flops 12288 | bytes 98304 | tf_op jit(solution)/shard_map/psum | solution.py:77
  1060.8 21.4 %fusion.11 = f32[1,384,1536]{2,1,0:T(8,128)} fusion(bf16[32,320,1536]{2,1,0:T(8,128)(2,1)} %select_convert_fusion, bf16[32,1,320,384]{3,2,1,0:T(8,128)(2,1)} %all_to_all.20), kind=kOutput, calls=%fused_computation.25 | convolution fusion | flops 12079595520 | bytes 41680896 | tf_op jit(solution)/shard_map/pecd,pecf->edf/dot_general | solution.py:64
  1082.2 23.9 %fusion.8 = f32[1,1536,384]{2,1,0:T(8,128)} fusion(bf16[32,320,1536]{2,1,0:T(8,128)(2,1)} %get-tuple-element.21, bf16[32,1,320,384]{3,2,1,0:T(8,128)(2,1)} %all_to_all.21), kind=kOutput, calls=%fused_computation.24 | convolution fusion | flops 12079595520 | bytes 41680896 | tf_op jit(solution)/shard_map/pecf,pecd->efd/dot_general | solution.py:63
  1106.2 36.9 %gather_fusion.2 = bf16[8192,384]{1,0:T(8,128)(2,1)} fusion(bf16[10240,384]{1,0:T(8,128)(2,1)} %bitcast.16, s32[8192]{0:T(1024)S(1)} %broadcast_clamp_fusion), kind=kCustom, calls=%fused_computation.1.clone | custom fusion | bytes 12615680 | tf_op jit(solution)/shard_map/jit(_take)/gather | solution.py:21
  1143.0 7.5 add_convert_fusion
  (33 shorter events, 8.6 us)
Async XLA Ops:
  0.6 277.6 %copy-start = (bf16[1,384,1536]{2,1,0:T(8,128)(2,1)S(1)}, bf16[1,384,1536]{2,1,0:T(8,128)(2,1)}, u32[]{:S(2)}) copy-start(bf16[1,384,1536]{2,1,0:T(8,128)(2,1)} %param.13) | copy-start | bytes 3538948
  14.9 557.6 %copy-start.4 = (pred[8192]{0:T(1024)(128)(4,1)}, pred[8192]{0:T(1024)(128)(4,1)S(1)}, u32[]{:S(2)}) copy-start(pred[8192]{0:T(1024)(128)(4,1)S(1)} %get-tuple-element.12) | copy-start | bytes 24580
  334.1 7.2 copy-start.2
  334.1 201.6 %all-to-all-start.3 = ((bf16[32,1,320,384]{3,2,1,0:T(8,128)(2,1)}), bf16[32,1,320,384]{3,2,1,0:T(8,128)(2,1)}, u32[]{:S(2)}, u32[]{:S(2)}) async-start(bf16[32,1,320,384]{3,2,1,0:T(8,128)(2,1)} %convert_bitcast_fusion), calls=%async_computation.3 | async-start | bytes 15728640 | tf_op jit(solution)/shard_map/all_to_all | solution.py:53
  341.3 5.1 copy-start.1
  863.8 242.4 %all-to-all-start.2 = ((bf16[32,1,320,384]{3,2,1,0:T(8,128)(2,1)}), bf16[32,1,320,384]{3,2,1,0:T(8,128)(2,1)}, u32[]{:S(2)}, u32[]{:S(2)}) async-start(bf16[32,1,320,384]{3,2,1,0:T(8,128)(2,1)} %convert_bitcast_fusion.1), calls=%async_computation.2 | async-start | bytes 15728640 | tf_op jit(solution)/shard_map/all_to_all | solution.py:66
  1106.2 36.9 %copy-start.3 = (f32[384,32]{0,1:T(8,128)S(1)}, f32[384,32]{0,1:T(8,128)}, u32[]{:S(2)}) copy-start(f32[384,32]{0,1:T(8,128)} %param.11) | copy-start | bytes 147460
  1106.2 36.9 %copy-start.5 = (pred[8192]{0:T(1024)(128)(4,1)S(1)}, pred[8192]{0:T(1024)(128)(4,1)}, u32[]{:S(2)}) copy-start(pred[8192]{0:T(1024)(128)(4,1)} %copy-done.4) | copy-start | bytes 24580
where the time goes:
time: 1160 us; the launch traced here: 1150 us
  blocking collectives  738 us (64%)
  local copies, waits for them, and re-layouts  193 us (17%)
  matrix products  169 us (15%)
  other arithmetic  37.6 us (3%)
    psum x1, blocking collectives, expert_layer(): lax.psum(jnp.einsum('sd,se->de', x_tokens, d_logits, preferred_element_ty...  188 us
    psum x1, blocking collectives, expert_layer(): route_stats = lax.psum(route_stats, 'ep')  186 us
    all_to_all x1, blocking collectives, expert_layer(): recv_rows = lax.all_to_all(sent_rows, 'ep', 0, 0, tiled=True)  184 us
    all_to_all x1, blocking collectives, expert_layer(): recv_grad = lax.all_to_all(sent_grad, 'ep', 0, 0, tiled=True)  180 us
    gather x4, local copies, waits for them, and re-layouts, gather_rows(): return jnp.take(source, row_index, axis=0, mode='fill', fill_value=0)  161 us
    dot_general x1, matrix products, expert_layer(): jnp.einsum('pecd,edf->pecf', recv_rows, w_in, preferred_element_type=jnp....  30.9 us
    scatter x1, local copies, waits for them, and re-layouts, route_slots(): jnp.full((n_slots,), tokens, jnp.int32).at[tok_slot]  30.5 us
    dot_general x1, matrix products, expert_layer(): jnp.einsum('pecd,efd->pecf', recv_grad, w_out, preferred_element_type=jnp...  26.8 us
  transfers between devices with their start and end apart: 2, of which 0 were waited for; matrix products, arithmetic and copies ran while one was open for 5% of the time, Pallas kernels for 0%

commit v1 on v0

v1 whole, which is shorter than its diff:
```python
import jax
import jax.numpy as jnp
from jax import lax
from jax.sharding import PartitionSpec as P

AUX_WEIGHT = 0.01
Z_WEIGHT = 0.001
BF = jnp.bfloat16
F32 = jnp.float32


def gather_rows(source, row_index):
    return jnp.take(source, row_index, axis=0, mode='fill', fill_value=0)


def solution(mesh):
    n_dev = mesh.shape['ep']
    hd = n_dev // 2
    groups = [list(range(hd)), list(range(hd, n_dev))]
    mirror = [(i, (i + hd) % n_dev) for i in range(n_dev)]

    def a2a(v):
        return lax.all_to_all(v, 'ep', 0, 0, tiled=True, axis_index_groups=groups)

    def expert_layer(x_tokens, w_router, expert_idx, w_in, w_out, grad_y):
        tokens, d_model = x_tokens.shape
        ne = n_dev
        capacity = (5 * tokens + 4 * ne - 1) // (4 * ne)
        total_tok = tokens * n_dev
        n_slots = ne * capacity
        me = lax.axis_index('ep')
        half = me // hd
        w_in_o, w_out_o = w_in[0], w_out[0]
        w_in_m = lax.ppermute(w_in_o, 'ep', mirror)
        w_out_m = lax.ppermute(w_out_o, 'ep', mirror)

        onehot = (expert_idx[:, None] == jnp.arange(ne, dtype=jnp.int32)[None, :]).astype(jnp.int32)
        position = jnp.sum(jnp.cumsum(onehot, axis=0) * onehot, axis=1) - 1
        rel = (expert_idx + hd * half) % ne
        kept = position < capacity
        tok_slot = jnp.where(kept, rel * capacity + position, n_slots)
        slot_tok = jnp.full((n_slots,), tokens, jnp.int32).at[tok_slot].set(jnp.arange(tokens, dtype=jnp.int32), mode='drop')
        counts = jnp.sum(onehot, axis=0).astype(F32)
        load_frac = lax.psum(counts, 'ep') / total_tok
        aux_vec = AUX_WEIGHT * ne * load_frac / total_tok
        z_coef = 2.0 * Z_WEIGHT / total_tok

        def router(rows):
            logits = jnp.dot(rows, w_router, preferred_element_type=F32)
            return jax.nn.softmax(logits, axis=-1), jax.nn.logsumexp(logits, axis=-1)

        def base_grad(p, lz):
            spread = jnp.sum(p * aux_vec, axis=-1, keepdims=True)
            return p * (aux_vec - spread) + (z_coef * lz)[:, None] * p

        def expert(xr, dyr, wi, wo, e_id):
            p, lz = router(xr)
            hot = (jnp.arange(ne) == e_id).astype(F32)
            gate = jnp.sum(p * hot, axis=-1)
            dyf = dyr.astype(F32)
            g = (gate[:, None] * dyf).astype(BF)
            h = jnp.maximum(jnp.dot(xr, wi, preferred_element_type=F32), 0.0).astype(BF)
            o = jnp.dot(h, wo, preferred_element_type=F32).astype(BF)
            dgate = jnp.sum(o.astype(F32) * dyf, axis=-1)
            dh = jnp.einsum('td,fd->tf', g, wo, preferred_element_type=F32)
            da = jnp.where(h > 0, dh, 0.0).astype(BF)
            gwo = jnp.einsum('tf,td->fd', h, g, preferred_element_type=F32)
            gwi = jnp.einsum('td,tf->df', xr, da, preferred_element_type=F32)
            dr = jnp.einsum('tf,df->td', da, wi, preferred_element_type=F32).astype(BF)
            dl = (gate * dgate)[:, None] * (hot - p) + base_grad(p, lz)
            gx = (dr.astype(F32) + jnp.einsum('te,de->td', dl, w_router)).astype(BF)
            gwr = jnp.einsum('td,te->de', xr, dl, preferred_element_type=F32)
            return gx, gwi, gwo, gwr

        hs = hd * capacity
        xm = a2a(gather_rows(x_tokens, slot_tok[hs:]))
        dym = a2a(gather_rows(grad_y, slot_tok[hs:]))
        xo = a2a(gather_rows(x_tokens, slot_tok[:hs]))
        dyo = a2a(gather_rows(grad_y, slot_tok[:hs]))
        gx_m, gwi_m, gwo_m, gwr_m = expert(xm, dym, w_in_m, w_out_m, (me + hd) % n_dev)
        gwi_r = lax.ppermute(gwi_m, 'ep', mirror)
        gwo_r = lax.ppermute(gwo_m, 'ep', mirror)
        back_m = a2a(gx_m)
        gx_o, gwi_o, gwo_o, gwr_o = expert(xo, dyo, w_in_o, w_out_o, me)
        back_o = a2a(gx_o)

        p, lz = router(x_tokens)
        dl = base_grad(p, lz)
        gx_drop = jnp.einsum('te,de->td', dl, w_router).astype(BF)
        gwr_d = jnp.einsum('td,te->de', x_tokens, jnp.where(kept[:, None], 0.0, dl), preferred_element_type=F32)
        back = jnp.concatenate([back_o, back_m], axis=0)
        rows = jnp.take(back, jnp.minimum(tok_slot, n_slots - 1), axis=0, mode='clip')
        grad_x = jnp.where(kept[:, None], rows, gx_drop)
        fin = jnp.concatenate([(gwr_d + gwr_m + gwr_o).reshape(-1), jnp.sum(p, axis=0), jnp.sum(lz * lz)[None]])
        fin = lax.psum(fin, 'ep')
        nr = d_model * ne
        grad_w_router = fin[:nr].reshape(d_model, ne)
        aux_loss = AUX_WEIGHT * ne * jnp.sum(load_frac * fin[nr:nr + ne] / total_tok)
        z_loss = Z_WEIGHT * fin[nr + ne] / total_tok
        return grad_x, (gwi_o + gwi_r)[None], (gwo_o + gwo_r)[None], grad_w_router, aux_loss, z_loss

    return jax.shard_map(expert_layer, mesh=mesh,
                         in_specs=(P('ep', None), P(None, None), P('ep'), P('ep', None, None), P('ep', None, None), P('ep', None)),
                         out_specs=(P('ep', None), P('ep', None, None), P('ep', None, None), P(None, None), P(), P()),
                         check_vma=False)
```

time: 1160 us -> 909 us (0.78)
  blocking collectives: 738 us -> 439 us
  matrix products: 169 us -> 193 us
  starting transfers between devices: 10.8 us -> 27.8 us
  other arithmetic: 37.6 us -> 50.1 us
    all_to_all x2, blocking collectives: 364 us -> 105 us  [a2a(): return lax.all_to_all(v, 'ep', 0, 0, tiled=True, axis_index_groups=groups)]
    gather x4, local copies, waits for them, and re-layouts: 161 us -> 97.1 us  [gather_rows(): return jnp.take(source, row_index, axis=0, mode='fill', fill_value=0)]
    psum x2, blocking collectives: 374 us -> 334 us  [the longest x1 207 us: expert_layer(): fin = lax.psum(fin, 'ep')]
    gather x0 -> x1, local copies, waits for them, and re-layouts: none -> 36.9 us  [expert_layer(): jnp.take(back, jnp.minimum(tok_slot, n_slots - 1), axis=0, mode='clip')]
    dot_general x9 -> x21, matrix products: 169 us -> 193 us  [the longest x2 33.8 us: expert(): dr = jnp.einsum('tf,df->td', da, wi, preferred_element_type=F32).astype(BF)]
    convert_element_type x0 -> x2, local copies, waits for them, and re-layouts: none -> 15.6 us  [expert(): dyf = dyr.astype(F32)]
    convert_element_type x1 -> x7, other arithmetic: 0.97 us -> 14.5 us  [the longest x2 7.61 us: expert(): g = (gate[:, None] * dyf).astype(BF)]
  transfers between devices with their start and end apart: 2 -> 8, of which waited for: 0 -> 0; matrix products, arithmetic and copies ran while one was open for 5% -> 24% of each run, Pallas kernels for 0% -> 0%
where the time goes in v1:
time: 909 us; the launch traced here: 901 us
  blocking collectives  439 us (48%)
  matrix products  193 us (21%)
  local copies, waits for them, and re-layouts  186 us (20%)
  other arithmetic  50.1 us (6%)
  starting transfers between devices  27.8 us (3%)
    psum x1, blocking collectives, expert_layer(): fin = lax.psum(fin, 'ep')  207 us
    psum x1, blocking collectives, expert_layer(): load_frac = lax.psum(counts, 'ep') / total_tok  126 us
    all_to_all x2, blocking collectives, a2a(): return lax.all_to_all(v, 'ep', 0, 0, tiled=True, axis_index_groups=groups)  105 us
    gather x4, local copies, waits for them, and re-layouts, gather_rows(): return jnp.take(source, row_index, axis=0, mode='fill', fill_value=0)  97.1 us
    gather x1, local copies, waits for them, and re-layouts, expert_layer(): jnp.take(back, jnp.minimum(tok_slot, n_slots - 1), axis=0, mode='clip')  36.9 us
    dot_general x2, matrix products, expert(): dr = jnp.einsum('tf,df->td', da, wi, preferred_element_type=F32).astype(BF)  33.8 us
    scatter x1, local copies, waits for them, and re-layouts, expert_layer(): jnp.full((n_slots,), tokens, jnp.int32).at[tok_slot]  30.5 us
    dot_general x2, matrix products, expert(): dh = jnp.einsum('td,fd->tf', g, wo, preferred_element_type=F32)  29 us
  transfers between devices with their start and end apart: 8, of which 0 were waited for; matrix products, arithmetic and copies ran while one was open for 24% of the time, Pallas kernels for 0%

profile of v1, /device:TPU:0, one launch (start us, length us, event | category | flops | bytes accessed | tf_op | source)
XLA Modules:
  0.0 901.1 jit_solution(10031982695726766523)
XLA Ops:
  14.1 30.5 %scatter_custom_fusion = s32[10240]{0:T(1024)S(1)} fusion(s32[8192]{0:T(1024)S(1)} %get-tuple-element.30, s32[8192]{0:T(1024)S(1)} %iota.21, s32[]{:T(128)} %constant.52.clone.1), kind=kCustom, calls=%fused_computation.116 | custom fusion | bytes 40964 | tf_op jit(solution)/shard_map/scatter | solution.py:42
  44.6 24.2 %gather_fusion.1 = bf16[5120,384]{1,0:T(8,128)(2,1)} fusion(bf16[8192,384]{1,0:T(8,128)(2,1)} %param.8, s32[5120]{0:T(1024)S(1)} %get-tuple-element.33), kind=kCustom, calls=%fused_computation.clone | custom fusion | bytes 7884800 | tf_op jit(solution)/shard_map/jit(_take)/gather | solution.py:13
  68.9 24.2 %gather_fusion.2 = bf16[5120,384]{1,0:T(8,128)(2,1)} fusion(bf16[8192,384]{1,0:T(8,128)(2,1)} %param.13, s32[5120]{0:T(1024)S(1)} %get-tuple-element.33), kind=kCustom, calls=%fused_computation.1.clone | custom fusion | bytes 7884800 | tf_op jit(solution)/shard_map/jit(_take)/gather | solution.py:13
  93.1 24.3 %gather_fusion.3 = bf16[5120,384]{1,0:T(8,128)(2,1)} fusion(bf16[8192,384]{1,0:T(8,128)(2,1)} %param.8, s32[5120]{0:T(1024)S(1)} %get-tuple-element.34), kind=kCustom, calls=%fused_computation.2.clone | custom fusion | bytes 7884800 | tf_op jit(solution)/shard_map/jit(_take)/gather | solution.py:13
  117.4 24.3 %gather_fusion.4 = bf16[5120,384]{1,0:T(8,128)(2,1)} fusion(bf16[8192,384]{1,0:T(8,128)(2,1)} %param.13, s32[5120]{0:T(1024)S(1)} %get-tuple-element.34), kind=kCustom, calls=%fused_computation.3.clone | custom fusion | bytes 7884800 | tf_op jit(solution)/shard_map/jit(_take)/gather | solution.py:13
  141.7 10.6 %broadcast_select_fusion = (bf16[5120,384]{1,0:T(8,128)(2,1)}, bf16[5120,384]{1,0:T(8,128)(2,1)S(1)}, bf16[5120,384]{1,0:T(8,128)(2,1)S(1)}, bf16[5120,384]{1,0:T(8,128)(2,1)}) fusion(bf16[5120,384]{1,0:T(8,128)(2,1)} %gather_fusion.4, pred[5120]{0:T(1024)(128)(4,1)S(1)} %get-tuple-element.32, bf16[5120,384]{1,0:T(8,128)(2,1)} %gather_fusion.3, ...), kind=kLoop, calls=%fused_computation.27 | loop fusion | flops 7864320 | bytes 31467520 | tf_op jit(solution)/shard_map/jit(_take)/select_n | solution.py:13
  152.4 55.0 %all_to_all.66 = bf16[16,320,384]{2,1,0:T(8,128)(2,1)} all-to-all(bf16[16,320,384]{2,1,0:T(8,128)(2,1)S(1)} %bitcast.93), channel_id=1, replica_groups={{0,1,2,3,4,5,6,7,8,9,10,11,12,13,14,15},{16,17,18,19,20,21,22,23,24,25,..., dimensions={0} | all-to-all | bytes 7864320 | tf_op jit(solution)/shard_map/all_to_all | solution.py:23
  207.4 50.3 %all_to_all.67 = bf16[16,320,384]{2,1,0:T(8,128)(2,1)} all-to-all(bf16[16,320,384]{2,1,0:T(8,128)(2,1)S(1)} %bitcast.92), channel_id=1, replica_groups={{0,1,2,3,4,5,6,7,8,9,10,11,12,13,14,15},{16,17,18,19,20,21,22,23,24,25,..., dimensions={0} | all-to-all | bytes 7864320 | tf_op jit(solution)/shard_map/all_to_all | solution.py:23
  265.5 126.4 %psum.14 = f32[32]{0:T(128)S(1)} all-reduce(f32[32]{0:T(128)S(1)} %convert_element_type.109), channel_id=1, replica_groups=mesh['ep'=32] {'ep'}, use_global_device_ids=true, to_apply=%region_9.11 | all-reduce | flops 32 | bytes 256 | tf_op jit(solution)/shard_map/psum | solution.py:44
  418.9 13.3 %maximum_convert_fusion.1 = bf16[5120,1536]{1,0:T(8,128)(2,1)} fusion(bf16[5120,384]{1,0:T(8,128)(2,1)} %bitcast.82, bf16[1,384,1536]{2,1,0:T(8,128)(2,1)S(1)} %copy-done.23), kind=kOutput, calls=%fused_computation.9 | convolution fusion | flops 6055526400 | bytes 20840448 | tf_op jit(solution)/shard_map/dot_general | solution.py:62
  432.2 11.0 %multiply_reduce_fusion.1 = f32[5120]{0:T(1024)S(1)} fusion(f32[5120,384]{0,1:T(8,128)} %copy.14, bf16[5120,1536]{1,0:T(8,128)(2,1)} %maximum_convert_fusion.1, bf16[1,1536,384]{2,1,0:T(8,128)(2,1)S(1)} %copy-done.24), kind=kOutput, calls=%fused_computation.18 | convolution fusion | flops 6047656960 | bytes 24793088 | tf_op jit(solution)/shard_map/dot_general | solution.py:63
  447.1 16.6 %select_convert_fusion.1 = bf16[5120,1536]{1,0:T(8,128)(2,1)} fusion(bf16[5120,1536]{1,0:T(8,128)(2,1)} %maximum_convert_fusion.1, bf16[5120,384]{1,0:T(8,128)(2,1)} %bitcast.95, bf16[1,1536,384]{2,1,0:T(8,128)(2,1)} %param.12), kind=kOutput, calls=%fused_computation.8 | convolution fusion | flops 6063390720 | bytes 36569088 | tf_op jit(solution)/shard_map/td,fd->tf/dot_general | solution.py:65
  463.7 12.2 %convolution_convert_fusion.4 = bf16[5120,384]{1,0:T(8,128)(2,1)S(1)} fusion(bf16[5120,1536]{1,0:T(8,128)(2,1)} %select_convert_fusion.1, bf16[1,384,1536]{2,1,0:T(8,128)(2,1)S(1)} %copy-done.23), kind=kOutput, calls=%fused_computation.23 | convolution fusion | flops 6041763840 | bytes 20840448 | tf_op jit(solution)/shard_map/tf,df->td/dot_general | solution.py:69
  490.2 12.4 %maximum_convert_fusion = bf16[5120,1536]{1,0:T(8,128)(2,1)} fusion(bf16[5120,384]{1,0:T(8,128)(2,1)S(1)} %bitcast.87, bf16[384,1536]{1,0:T(8,128)(2,1)} %collective-permute-done), kind=kOutput, calls=%fused_computation.7 | convolution fusion | flops 6055526400 | bytes 20840448 | tf_op jit(solution)/shard_map/dot_general | solution.py:62
  511.6 11.4 %multiply_reduce_fusion = f32[5120]{0:T(1024)S(1)} fusion(f32[5120,384]{0,1:T(8,128)} %copy.15, bf16[5120,1536]{1,0:T(8,128)(2,1)} %maximum_convert_fusion, bf16[1536,384]{1,0:T(8,128)(2,1)} %collective-permute-done.1), kind=kOutput, calls=%fused_computation.15 | convolution fusion | flops 6047656960 | bytes 24793088 | tf_op jit(solution)/shard_map/dot_general | solution.py:63
  533.2 12.4 %fusion.72 = bf16[5120,1536]{1,0:T(8,128)(2,1)} fusion(bf16[5120,384]{1,0:T(8,128)(2,1)S(1)} %multiply_convert_fusion.1, bf16[1536,384]{1,0:T(8,128)(2,1)} %collective-permute-done.1), kind=kOutput, calls=%fused_computation.140 | convolution fusion | flops 6039797760 | bytes 20840448 | tf_op jit(solution)/shard_map/td,fd->tf/dot_general | solution.py:65
  545.6 21.5 %add_convert_fusion = bf16[5120,384]{1,0:T(8,128)(2,1)} fusion(f32[5120,384]{1,0:T(8,128)} %fusion.24, bf16[384,1536]{1,0:T(8,128)(2,1)} %collective-permute-done, bf16[5120,1536]{1,0:T(8,128)(2,1)} %fusion.72, bf16[5120,1536]{1,0:T(8,128)(2,1)} %maximum_convert_fusion), kind=kOutput, calls=%fused_computation.14 | convolution fusion | flops 6079119360 | bytes 44433408 | tf_op jit(solution)/shard_map/tf,df->td/dot_general | solution.py:69
  572.3 14.0 %fusion.73 = f32[1536,384]{1,0:T(8,128)} fusion(bf16[5120,1536]{1,0:T(8,128)(2,1)} %maximum_convert_fusion, bf16[5120,384]{1,0:T(8,128)(2,1)} %copy-done.9), kind=kOutput, calls=%fused_computation.141 | convolution fusion | flops 6039797760 | bytes 22020096 | tf_op jit(solution)/shard_map/tf,td->fd/dot_general | solution.py:67
  587.6 15.0 %fusion.67 = f32[384,1536]{1,0:T(8,128)} fusion(bf16[5120,384]{1,0:T(8,128)(2,1)S(1)} %bitcast.88, bf16[5120,1536]{1,0:T(8,128)(2,1)} %fusion.72, bf16[5120,1536]{1,0:T(8,128)(2,1)} %maximum_convert_fusion), kind=kOutput, calls=%fused_computation.135 | convolution fusion | flops 6071255040 | bytes 37748736 | tf_op jit(solution)/shard_map/td,tf->df/dot_general | solution.py:68
  606.7 207.5 %psum.15 = f32[12321]{0:T(1024)S(1)} all-reduce(f32[12321]{0:T(1024)S(1)} %concatenate.7), channel_id=1, replica_groups=mesh['ep'=32] {'ep'}, use_global_device_ids=true, to_apply=%region_24.26 | all-reduce | flops 12321 | bytes 98568 | tf_op jit(solution)/shard_map/psum | solution.py:95
  817.6 14.6 %fusion.4 = f32[1,1536,384]{2,1,0:T(8,128)} fusion(f32[1536,384]{1,0:T(8,128)} %collective-permute-done.3, bf16[5120,1536]{1,0:T(8,128)(2,1)} %maximum_convert_fusion.1, f32[5120]{0:T(1024)S(1)} %get-tuple-element.25, bf16[5120,384]{1,0:T(8,128)(2,1)} %bitcast.49), kind=kOutput, calls=%fused_computation.33 | convolution fusion | flops 6046285824 | bytes 24399872 | tf_op jit(solution)/shard_map/tf,td->fd/dot_general | solution.py:67
  832.2 12.3 %fusion.5 = f32[1,384,1536]{2,1,0:T(8,128)} fusion(f32[384,1536]{1,0:T(8,128)} %collective-permute-done.2, bf16[5120,384]{1,0:T(8,128)(2,1)S(1)} %bitcast.85, bf16[5120,1536]{1,0:T(8,128)(2,1)} %select_convert_fusion.1), kind=kOutput, calls=%fused_computation.34 | convolution fusion | flops 6040387584 | bytes 24379392 | tf_op jit(solution)/shard_map/td,tf->df/dot_general | solution.py:68
  844.5 9.8 %pad_maximum_fusion = bf16[10240,384]{1,0:T(8,128)(2,1)} fusion(bf16[5120,384]{1,0:T(8,128)(2,1)} %bitcast.17, bf16[5120,384]{1,0:T(8,128)(2,1)} %bitcast.10), kind=kLoop, calls=%fused_computation.12 | loop fusion | flops 15728640 | bytes 15728640 | tf_op jit(solution)/shard_map/concatenate | solution.py:91
  854.3 36.9 %gather_fusion = bf16[8192,384]{1,0:T(8,128)(2,1)} fusion(bf16[10240,384]{1,0:T(8,128)(2,1)} %pad_maximum_fusion, s32[8192]{0:T(1024)S(1)} %copy-done.13), kind=kCustom, calls=%fused_computation.4 | custom fusion | bytes 12615680 | tf_op jit(solution)/shard_map/jit(_take)/gather | solution.py:92
  (128 shorter events, 105.4 us)
Async XLA Ops:
  0.6 391.3 %copy-start = (f32[384,32]{0,1:T(8,128)S(1)}, f32[384,32]{0,1:T(8,128)}, u32[]{:S(2)}) copy-start(f32[384,32]{0,1:T(8,128)} %param.9) | copy-start | bytes 147460
  0.6 12.0 %copy-start.12 = (s32[8192]{0:T(1024)S(1)}, s32[8192]{0:T(1024)}, u32[]{:S(2)}) copy-start(s32[8192]{0:T(1024)} %param.10) | copy-start | bytes 98308
  257.7 141.3 %slice-start = ((s8[6291456]{0:T(1024)(128)(4,1)}), s8[2097152]{0:T(1024)(128)(4,1)S(1)}, s32[]{:S(2)}) async-start(s8[6291456]{0:T(1024)(128)(4,1)} %bitcast.80), calls=%async_computation.6 | async-start | bytes 4194304
  257.7 146.8 %all-to-all-start.1 = ((bf16[16,320,384]{2,1,0:T(8,128)(2,1)}), bf16[16,320,384]{2,1,0:T(8,128)(2,1)}, u32[]{:S(2)}, u32[]{:S(2)}) async-start(bf16[16,320,384]{2,1,0:T(8,128)(2,1)} %bitcast.91), calls=%async_computation.1 | async-start | bytes 7864320 | tf_op jit(solution)/shard_map/all_to_all | solution.py:23
  262.5 227.7 %collective-permute-start = (bf16[384,1536]{1,0:T(8,128)(2,1)S(1)}, bf16[384,1536]{1,0:T(8,128)(2,1)}, u32[]{:S(2)}, u32[]{:S(2)}) collective-permute-start(bf16[384,1536]{1,0:T(8,128)(2,1)S(1)} %bitcast.100), channel_id=1, source_target_pairs={{0,16},{1,17},{2,18},{3,19},{4,20},{5,21},{6,22},{7,23},{8,24},{9,... | collective-permute-start | bytes 3538952 | tf_op jit(solution)/shard_map/ppermute | solution.py:34
  265.1 246.5 %collective-permute-start.1 = (bf16[1536,384]{1,0:T(8,128)(2,1)}, bf16[1536,384]{1,0:T(8,128)(2,1)}, u32[]{:S(2)}, u32[]{:S(2)}) collective-permute-start(bf16[1536,384]{1,0:T(8,128)(2,1)} %bitcast.101), channel_id=1, source_target_pairs={{0,16},{1,17},{2,18},{3,19},{4,20},{5,21},{6,22},{7,23},{8,24},{9,... | collective-permute-start | bytes 3538952 | tf_op jit(solution)/shard_map/ppermute | solution.py:35
  391.9 7.1 slice-start.1
  404.5 74.6 %all-to-all-start.4 = ((bf16[16,320,384]{2,1,0:T(8,128)(2,1)}), bf16[16,320,384]{2,1,0:T(8,128)(2,1)}, u32[]{:S(2)}, u32[]{:S(2)}) async-start(bf16[16,320,384]{2,1,0:T(8,128)(2,1)} %bitcast.90), calls=%async_computation.4 | async-start | bytes 7864320 | tf_op jit(solution)/shard_map/all_to_all | solution.py:23
  418.9 13.3 %copy-start.24 = (bf16[1,1536,384]{2,1,0:T(8,128)(2,1)S(1)}, bf16[1,1536,384]{2,1,0:T(8,128)(2,1)}, u32[]{:S(2)}) copy-start(bf16[1,1536,384]{2,1,0:T(8,128)(2,1)} %param.12) | copy-start | bytes 3538948
  479.2 88.0 %all-to-all-start.2 = ((bf16[16,320,384]{2,1,0:T(8,128)(2,1)}), bf16[16,320,384]{2,1,0:T(8,128)(2,1)}, u32[]{:S(2)}, u32[]{:S(2)}) async-start(bf16[16,320,384]{2,1,0:T(8,128)(2,1)} %bitcast.97), calls=%async_computation.2 | async-start | bytes 7864320 | tf_op jit(solution)/shard_map/all_to_all | solution.py:23
  567.1 277.3 %all-to-all-start.5 = ((bf16[16,320,384]{2,1,0:T(8,128)(2,1)}), bf16[16,320,384]{2,1,0:T(8,128)(2,1)}, u32[]{:S(2)}, u32[]{:S(2)}) async-start(bf16[16,320,384]{2,1,0:T(8,128)(2,1)} %bitcast.96), calls=%async_computation.5 | async-start | bytes 7864320 | tf_op jit(solution)/shard_map/all_to_all | solution.py:23
  572.2 15.4 %copy-start.6 = (bf16[16,320,384]{2,1,0:T(8,128)(2,1)S(1)}, bf16[16,320,384]{2,1,0:T(8,128)(2,1)}, u32[]{:S(2)}) copy-start(bf16[16,320,384]{2,1,0:T(8,128)(2,1)} %all_to_all.66) | copy-start | bytes 11796484
  586.3 17.9 %copy-start.27 = (f32[384,32]{0,1:T(8,128)S(1)}, f32[384,32]{0,1:T(8,128)}, u32[]{:S(2)}) copy-start(f32[384,32]{0,1:T(8,128)} %convolution_bitcast_fusion) | copy-start | bytes 147460
  586.3 231.3 %collective-permute-start.3 = (f32[1536,384]{1,0:T(8,128)}, f32[1536,384]{1,0:T(8,128)}, u32[]{:S(2)}, u32[]{:S(2)}) collective-permute-start(f32[1536,384]{1,0:T(8,128)} %fusion.73), channel_id=1, source_target_pairs={{0,16},{1,17},{2,18},{3,19},{4,20},{5,21},{6,22},{7,23},{8,24},{9,... | collective-permute-start | bytes 7077896 | tf_op jit(solution)/shard_map/ppermute | solution.py:82
  602.6 229.6 %collective-permute-start.2 = (f32[384,1536]{1,0:T(8,128)}, f32[384,1536]{1,0:T(8,128)}, u32[]{:S(2)}, u32[]{:S(2)}) collective-permute-start(f32[384,1536]{1,0:T(8,128)} %fusion.67), channel_id=1, source_target_pairs={{0,16},{1,17},{2,18},{3,19},{4,20},{5,21},{6,22},{7,23},{8,24},{9,... | collective-permute-start | bytes 7077896 | tf_op jit(solution)/shard_map/ppermute | solution.py:81
  605.0 210.7 %copy-start.26 = (f32[32]{0:T(128)S(1)}, f32[32]{0:T(128)}, u32[]{:S(2)}) copy-start(f32[32]{0:T(128)} %copy-done.25) | copy-start | bytes 388
  817.6 14.6 %copy-start.3 = (bf16[16,320,384]{2,1,0:T(8,128)(2,1)S(1)}, bf16[16,320,384]{2,1,0:T(8,128)(2,1)}, u32[]{:S(2)}) copy-start(bf16[16,320,384]{2,1,0:T(8,128)(2,1)} %all_to_all.67) | copy-start | bytes 11796484
  844.5 9.8 %copy-start.13 = (s32[8192]{0:T(1024)S(1)}, s32[8192]{0:T(1024)}, u32[]{:S(2)}) copy-start(s32[8192]{0:T(1024)} %get-tuple-element.29) | copy-start | bytes 98308
  854.2 37.0 %copy-start.8 = (f32[8192,32]{0,1:T(8,128)S(1)}, f32[8192,32]{0,1:T(8,128)}, u32[]{:S(2)}) copy-start(f32[8192,32]{0,1:T(8,128)} %copy-done.7) | copy-start | bytes 3145732
  854.2 37.0 %copy-start.11 = (f32[8192]{0:T(1024)S(1)}, f32[8192]{0:T(1024)}, u32[]{:S(2)}) copy-start(f32[8192]{0:T(1024)} %copy-done.10) | copy-start | bytes 98308
  854.2 37.0 %copy-start.15 = (f32[8192]{0:T(1024)S(1)}, f32[8192]{0:T(1024)}, u32[]{:S(2)}) copy-start(f32[8192]{0:T(1024)} %copy-done.14) | copy-start | bytes 98308
  854.3 36.9 %copy-start.17 = (f32[8192]{0:T(1024)S(1)}, f32[8192]{0:T(1024)}, u32[]{:S(2)}) copy-start(f32[8192]{0:T(1024)} %copy-done.16) | copy-start | bytes 98308
  854.3 36.9 %copy-start.19 = (f32[8192]{0:T(1024)S(1)}, f32[8192]{0:T(1024)}, u32[]{:S(2)}) copy-start(f32[8192]{0:T(1024)} %copy-done.18) | copy-start | bytes 98308
  854.3 36.9 %copy-start.21 = (pred[8192]{0:T(1024)(128)(4,1)S(1)}, pred[8192]{0:T(1024)(128)(4,1)}, u32[]{:S(2)}) copy-start(pred[8192]{0:T(1024)(128)(4,1)} %copy-done.20) | copy-start | bytes 24580
  (14 other events, 45.0 us)

commit v2 on v1

v2 whole, which is shorter than its diff:
```python
import functools
import jax
import jax.numpy as jnp
from jax import lax
from jax.experimental import pallas as pl
from jax.experimental.pallas import tpu as pltpu
from jax.sharding import PartitionSpec as P

AUX_WEIGHT = 0.01
Z_WEIGHT = 0.001
BF = jnp.bfloat16
F32 = jnp.float32
LANES = 128
MESH_ID = pl.DeviceIdType.MESH
VMEM_LIMIT = 60 * 1024 * 1024


def gather_rows(source, row_index):
    return jnp.take(source, row_index, axis=0, mode='fill', fill_value=0)


def xor3(a, b):
    out = 0
    for k in (1, 2, 4):
        out = out + k * lax.rem(a // k + b // k, 2)
    return out


def dot(a, b, ca=1, cb=0):
    return lax.dot_general(a, b, (((ca,), (cb,)), ((), ())), preferred_element_type=F32)


def expert_kernel(cfg, *refs):
    n_dev, hd, cap, d, ff, ft, total_tok, first = cfg
    if first:
        (cnt_ref, sx, sdy, wi, wo, wr, wrt,
         gx_out, gwi, gwo, gwr, tot_ref,
         xr, dyr, gwot, dlw, oacc, dracc, gb, xt, gt, stage,
         cbuf, csend, crecv, loc_sem, send_sem, recv_sem, out_sem) = refs
    else:
        (tot_in, gxm, sx, sdy, wi, wo, wr, wrt,
         back_m, back_o, gwi, gwo, gwr,
         xr, dyr, gwot, dlw, oacc, dracc, gb, xt, gt, stage,
         loc_sem, send_sem, recv_sem, out_sem, bm_send, bm_recv, bo_send, bo_recv) = refs
    me = lax.axis_index('ep')
    half = me // hd
    rank = lax.rem(me, hd)
    chip = rank // 2
    core = lax.rem(rank, 2)
    n_grp = hd // 2
    rows = 2 * cap

    def peer_of(j, c):
        return xor3(chip, j) * 2 + lax.rem(core + c, 2)

    def token_copy(a, src, dst, peer):
        return pltpu.make_async_remote_copy(
            src_ref=src.at[peer], dst_ref=dst.at[rank], send_sem=send_sem.at[a, peer],
            recv_sem=recv_sem.at[a, rank], device_id=(half * hd + peer,), device_id_type=MESH_ID)

    def token_wait(a, src, dst, peer):
        return pltpu.make_async_remote_copy(
            src_ref=src.at[peer], dst_ref=dst.at[peer], send_sem=send_sem.at[a, peer],
            recv_sem=recv_sem.at[a, peer], device_id=(half * hd + peer,), device_id_type=MESH_ID)

    def back_copy(src, dst, ssem, rsem, peer):
        return pltpu.make_async_remote_copy(
            src_ref=src.at[peer], dst_ref=dst.at[rank], send_sem=ssem.at[peer],
            recv_sem=rsem.at[rank], device_id=(half * hd + peer,), device_id_type=MESH_ID)

    def back_wait(src, dst, ssem, rsem, peer):
        return pltpu.make_async_remote_copy(
            src_ref=src.at[peer], dst_ref=dst.at[peer], send_sem=ssem.at[peer],
            recv_sem=rsem.at[peer], device_id=(half * hd + peer,), device_id_type=MESH_ID)

    if first:
        def count_send(k):
            peer = lax.rem(me + k, n_dev)
            return pltpu.make_async_remote_copy(
                src_ref=cnt_ref, dst_ref=cbuf.at[me], send_sem=csend.at[peer],
                recv_sem=crecv.at[me], device_id=(peer,), device_id_type=MESH_ID)

        def count_wait(k):
            peer = lax.rem(me + k, n_dev)
            return pltpu.make_async_remote_copy(
                src_ref=cnt_ref, dst_ref=cbuf.at[peer], send_sem=csend.at[peer],
                recv_sem=crecv.at[peer], device_id=(peer,), device_id_type=MESH_ID)

        def start_count(k, _):
            count_send(k).start()
            return 0
        lax.fori_loop(1, n_dev, start_count, 0)
        cbuf[me] = cnt_ref[...]

    own_x = pltpu.make_async_copy(sx.at[rank], xr.at[rank], loc_sem.at[0])
    own_dy = pltpu.make_async_copy(sdy.at[rank], dyr.at[rank], loc_sem.at[1])
    own_x.start()
    own_dy.start()

    def start_peer(peer):
        token_copy(0, sx, xr, peer).start()
        token_copy(1, sdy, dyr, peer).start()
        if not first:
            back_copy(gxm, back_m, bm_send, bm_recv, peer).start()

    start_peer(peer_of(0, 1))

    def start_group(j, _):
        start_peer(peer_of(j, 0))
        start_peer(peer_of(j, 1))
        return 0
    lax.fori_loop(1, n_grp, start_group, 0)
    if not first:
        own_bm = pltpu.make_async_copy(gxm.at[rank], back_m.at[rank], loc_sem.at[2])
        own_bm.start()

    gwi[...] = jnp.zeros_like(gwi)
    gwot[...] = jnp.zeros_like(gwot)
    gwr[...] = jnp.zeros_like(gwr)

    if first:
        def wait_count(k, _):
            count_wait(k).wait_recv()
            return 0
        lax.fori_loop(1, n_dev, wait_count, 0)
        tot_ref[...] = jnp.sum(cbuf[...], axis=0)
        tot = tot_ref[0:1, :]
        e_id = lax.rem(me + hd, n_dev)
    else:
        tot = tot_in[0:1, :]
        e_id = me
    v = tot * (AUX_WEIGHT * n_dev / (float(total_tok) * total_tok))
    zc = 2.0 * Z_WEIGHT / total_tok

    def group(j, _):
        @pl.when(j == 0)
        def _():
            own_x.wait()
            own_dy.wait()

        @pl.when(j > 0)
        def _():
            token_wait(0, sx, xr, peer_of(j, 0)).wait_recv()
            token_wait(1, sdy, dyr, peer_of(j, 0)).wait_recv()
        token_wait(0, sx, xr, peer_of(j, 1)).wait_recv()
        token_wait(1, sdy, dyr, peer_of(j, 1)).wait_recv()
        pair = xor3(chip, j)
        x = xr[pl.ds(2 * pair, 2)].reshape(rows, d)
        dyf = dyr[pl.ds(2 * pair, 2)].reshape(rows, d).astype(F32)
        lane = lax.broadcasted_iota(jnp.int32, (rows, LANES), 1)
        lg = dot(x, wr[...])
        lg = lg[:, :LANES] + lg[:, LANES:]
        lg = jnp.where(lane < n_dev, lg, -1e30)
        mx = jnp.max(lg, axis=1, keepdims=True)
        ex = jnp.exp(lg - mx)
        sm = jnp.sum(ex, axis=1, keepdims=True)
        p = ex / sm
        lz = mx + jnp.log(sm)
        hot = (lane == e_id).astype(F32)
        gate = jnp.sum(p * hot, axis=1, keepdims=True)
        g = (gate * dyf).astype(BF)
        gb[...] = g
        xt[...] = x.T
        gt[...] = g.T
        oacc[...] = jnp.zeros_like(oacc)
        dracc[...] = jnp.zeros_like(dracc)

        def ff_tile(f, _):
            fo = pl.multiple_of(f * ft, ft)
            wit = wi[:, pl.ds(fo, ft)]
            wot = wo[pl.ds(fo, ft), :]
            xx = xr[pl.ds(2 * pair, 2)].reshape(rows, d)
            h = jnp.maximum(dot(xx, wit), 0.0).astype(BF)
            oacc[...] += dot(h, wot)
            dh = dot(gb[...], wot, 1, 1)
            da = jnp.where(h > 0, dh, 0.0).astype(BF)
            dracc[...] += dot(da, wit, 1, 1)
            gwot[:, pl.ds(fo, ft)] += dot(gt[...], h)
            gwi[:, pl.ds(fo, ft)] += dot(xt[...], da)
            return 0
        lax.fori_loop(0, ff // ft, ff_tile, 0)

        o = oacc[...].astype(BF).astype(F32)
        dgate = jnp.sum(o * dyf, axis=1, keepdims=True)
        spread = jnp.sum(p * v, axis=1, keepdims=True)
        dl = (gate * dgate) * (hot - p) + p * (v - spread) + (zc * lz) * p
        dl_hi = dl.astype(BF)
        dl_lo = (dl - dl_hi.astype(F32)).astype(BF)
        dl2 = jnp.concatenate([dl_hi, dl_lo], axis=1)
        dlw[...] = dot(jnp.concatenate([dl2, dl_hi], axis=1), wrt[...])
        gw = dot(xt[...], dl2)
        gwr[...] += gw[:, :LANES] + gw[:, LANES:]
        gx = (dracc[...].astype(BF).astype(F32) + dlw[...]).astype(BF)
        stage[pl.ds(2 * pair, 2)] = gx.reshape(2, cap, d)
        for c in (0, 1):
            peer = peer_of(j, c)
            if first:
                pltpu.make_async_copy(stage.at[peer], gx_out.at[peer], out_sem.at[peer]).start()
            elif c == 1:
                back_copy(stage, back_o, bo_send, bo_recv, peer).start()
            else:
                @pl.when(j == 0)
                def _():
                    pltpu.make_async_copy(stage.at[rank], back_o.at[rank], out_sem.at[0]).start()

                @pl.when(j > 0)
                def _():
                    back_copy(stage, back_o, bo_send, bo_recv, peer).start()
        return 0
    lax.fori_loop(0, n_grp, group, 0)

    def finish(f, _):
        fo = pl.multiple_of(f * ft, ft)
        gwo[pl.ds(fo, ft), :] = gwot[:, pl.ds(fo, ft)].T
        return 0
    lax.fori_loop(0, ff // ft, finish, 0)

    def drain_peer(peer):
        token_wait(0, sx, xr, peer).wait_send()
        token_wait(1, sdy, dyr, peer).wait_send()
        if not first:
            back_wait(gxm, back_m, bm_send, bm_recv, peer).wait_send()
            back_wait(gxm, back_m, bm_send, bm_recv, peer).wait_recv()
            back_wait(stage, back_o, bo_send, bo_recv, peer).wait_send()
            back_wait(stage, back_o, bo_send, bo_recv, peer).wait_recv()

    drain_peer(peer_of(0, 1))

    def drain(j, _):
        drain_peer(peer_of(j, 0))
        drain_peer(peer_of(j, 1))
        return 0
    lax.fori_loop(1, n_grp, drain, 0)
    if first:
        def out_wait(s, _):
            pltpu.make_async_copy(stage.at[s], gx_out.at[s], out_sem.at[s]).wait()
            return 0
        lax.fori_loop(0, hd, out_wait, 0)

        def count_drain(k, _):
            count_wait(k).wait_send()
            return 0
        lax.fori_loop(1, n_dev, count_drain, 0)
    else:
        own_bm.wait()
        pltpu.make_async_copy(stage.at[rank], back_o.at[rank], out_sem.at[0]).wait()


def expert_call(cfg, *args):
    n_dev, hd, cap, d, ff, ft, total_tok, first = cfg
    vm = pl.BlockSpec(memory_space=pltpu.VMEM)
    hbm = pl.BlockSpec(memory_space=pltpu.HBM)
    sd = jax.ShapeDtypeStruct
    rows = 2 * cap
    tok = sd((hd, cap, d), BF)
    grads = [sd((d, ff), F32), sd((ff, d), F32), sd((d, LANES), F32)]
    dma = pltpu.SemaphoreType.DMA
    scratch = [pltpu.VMEM((hd, cap, d), BF), pltpu.VMEM((hd, cap, d), BF), pltpu.VMEM((d, ff), F32),
               pltpu.VMEM((rows, d), F32), pltpu.VMEM((rows, d), F32), pltpu.VMEM((rows, d), F32),
               pltpu.VMEM((rows, d), BF), pltpu.VMEM((d, rows), BF), pltpu.VMEM((d, rows), BF),
               pltpu.VMEM((hd, cap, d), BF)]
    common = [dma((3,)), dma((2, hd)), dma((2, hd)), dma((hd,))]
    if first:
        in_specs = [vm, hbm, hbm, vm, vm, vm, vm]
        out_shape = [tok] + grads + [sd((8, LANES), F32)]
        out_specs = [hbm, vm, vm, vm, vm]
        scratch += [pltpu.VMEM((n_dev, 8, LANES), F32), dma((n_dev,)), dma((n_dev,))] + common
    else:
        in_specs = [vm, hbm, hbm, hbm, vm, vm, vm, vm]
        out_shape = [tok, tok] + grads
        out_specs = [hbm, hbm, vm, vm, vm]
        scratch += common + [dma((hd,))] * 4
    return pl.pallas_call(
        functools.partial(expert_kernel, cfg), out_shape=out_shape, in_specs=in_specs, out_specs=out_specs,
        scratch_shapes=scratch, name='expert_a' if first else 'expert_b',
        cost_estimate=pl.CostEstimate(flops=12 * hd * cap * d * ff, bytes_accessed=32 * 2 ** 20, transcendentals=0),
        compiler_params=pltpu.CompilerParams(has_side_effects=True, vmem_limit_bytes=VMEM_LIMIT))(*args)


def split_router(w_router):
    d, ne = w_router.shape
    hi = lax.reduce_precision(w_router, 8, 7)
    lo = lax.reduce_precision(w_router - hi, 8, 7)
    pad = lambda a: jnp.pad(a, ((0, 0), (0, LANES - ne)))
    wr = jnp.concatenate([pad(hi), pad(lo)], axis=1).astype(BF)
    wrt = jnp.concatenate([pad(hi), pad(hi), pad(lo)], axis=1).T.astype(BF)
    return wr, wrt


def solution(mesh):
    n_dev = mesh.shape['ep']
    hd = n_dev // 2
    mirror = [(i, (i + hd) % n_dev) for i in range(n_dev)]

    def expert_layer(x_tokens, w_router, expert_idx, w_in, w_out, grad_y):
        tokens, d_model = x_tokens.shape
        ff = w_in.shape[-1]
        ne = n_dev
        capacity = (5 * tokens + 4 * ne - 1) // (4 * ne)
        total_tok = tokens * n_dev
        n_slots = ne * capacity
        me = lax.axis_index('ep')
        half = me // hd
        w_in_o, w_out_o = w_in[0], w_out[0]
        w_in_m = lax.ppermute(w_in_o, 'ep', mirror)
        w_out_m = lax.ppermute(w_out_o, 'ep', mirror)
        wr, wrt = split_router(w_router)

        onehot = (expert_idx[:, None] == jnp.arange(ne, dtype=jnp.int32)[None, :]).astype(jnp.int32)
        position = jnp.sum(jnp.cumsum(onehot, axis=0) * onehot, axis=1) - 1
        rel = (expert_idx + hd * half) % ne
        kept = position < capacity
        tok_slot = jnp.where(kept, rel * capacity + position, n_slots)
        slot_tok = jnp.full((n_slots,), tokens, jnp.int32).at[tok_slot].set(jnp.arange(tokens, dtype=jnp.int32), mode='drop')
        counts = jnp.sum(onehot, axis=0).astype(F32)
        cnt = jnp.broadcast_to(jnp.pad(counts, (0, LANES - ne))[None], (8, LANES))

        hs = hd * capacity
        shape = (hd, capacity, d_model)
        base = (n_dev, hd, capacity, d_model, ff, 512, total_tok)
        xm = gather_rows(x_tokens, slot_tok[hs:]).reshape(shape)
        dym = gather_rows(grad_y, slot_tok[hs:]).reshape(shape)
        gx_m, gwi_m, gwo_m, gwr_m, tot = expert_call(base + (True,), cnt, xm, dym, w_in_m, w_out_m, wr, wrt)
        gwi_r = lax.ppermute(gwi_m, 'ep', mirror)
        gwo_r = lax.ppermute(gwo_m, 'ep', mirror)
        xo = gather_rows(x_tokens, slot_tok[:hs]).reshape(shape)
        dyo = gather_rows(grad_y, slot_tok[:hs]).reshape(shape)
        back_m, back_o, gwi_o, gwo_o, gwr_o = expert_call(base + (False,), tot, gx_m, xo, dyo, w_in_o, w_out_o, wr, wrt)

        load_frac = tot[0, :ne] / total_tok
        aux_vec = AUX_WEIGHT * ne * load_frac / total_tok
        z_coef = 2.0 * Z_WEIGHT / total_tok
        logits = jnp.dot(x_tokens, w_router, preferred_element_type=F32)
        p = jax.nn.softmax(logits, axis=-1)
        lz = jax.nn.logsumexp(logits, axis=-1)
        dl = p * (aux_vec - jnp.sum(p * aux_vec, axis=-1, keepdims=True)) + (z_coef * lz)[:, None] * p
        gx_drop = jnp.einsum('te,de->td', dl, w_router).astype(BF)
        gwr_d = jnp.einsum('td,te->de', x_tokens, jnp.where(kept[:, None], 0.0, dl), preferred_element_type=F32)
        back = jnp.concatenate([back_o, back_m], axis=0).reshape(n_slots, d_model)
        rows = jnp.take(back, jnp.minimum(tok_slot, n_slots - 1), axis=0, mode='clip')
        grad_x = jnp.where(kept[:, None], rows, gx_drop)
        fin = jnp.concatenate([(gwr_d + (gwr_m + gwr_o)[:, :ne]).reshape(-1), jnp.sum(p, axis=0), jnp.sum(lz * lz)[None]])
        fin = lax.psum(fin, 'ep')
        nr = d_model * ne
        grad_w_router = fin[:nr].reshape(d_model, ne)
        aux_loss = AUX_WEIGHT * ne * jnp.sum(load_frac * fin[nr:nr + ne] / total_tok)
        z_loss = Z_WEIGHT * fin[nr + ne] / total_tok
        return grad_x, (gwi_o + gwi_r)[None], (gwo_o + gwo_r)[None], grad_w_router, aux_loss, z_loss

    return jax.shard_map(expert_layer, mesh=mesh,
                         in_specs=(P('ep', None), P(None, None), P('ep'), P('ep', None, None), P('ep', None, None), P('ep', None)),
                         out_specs=(P('ep', None), P('ep', None, None), P('ep', None, None), P(None, None), P(), P()),
                         check_vma=False)
```

time: 909 us -> 720 us (0.79)
  Pallas kernels: 0 us -> 435 us
  blocking collectives: 439 us -> 40.3 us
  matrix products: 193 us -> 18 us
  starting transfers between devices: 27.8 us -> 7.17 us
  local copies, waits for them, and re-layouts: 186 us -> 173 us
    pallas_call x0 -> x2, Pallas kernels: none -> 435 us  [expert_call(): pl.pallas_call(functools.partial(expert_kernel, cfg), out_shape=out_shape...]
    dot_general x19 -> x1, matrix products: 183 us -> 4.82 us  [expert_layer(): logits = jnp.dot(x_tokens, w_router, preferred_element_type=F32)]
    psum x1, blocking collectives: 207 us -> 40.3 us  [expert_layer(): fin = lax.psum(fin, 'ep')]
    psum x1 -> x0, blocking collectives: 126 us -> none  [expert_layer(): load_frac = lax.psum(counts, 'ep') / total_tok]
    all_to_all x2 -> x0, blocking collectives: 105 us -> none  [a2a(): return lax.all_to_all(v, 'ep', 0, 0, tiled=True, axis_index_groups=groups)]
    all_to_all x4 -> x0, starting transfers between devices: 21.9 us -> none  [a2a(): return lax.all_to_all(v, 'ep', 0, 0, tiled=True, axis_index_groups=groups)]
    convert_element_type x2 -> x0, local copies, waits for them, and re-layouts: 15.6 us -> none  [expert(): dyf = dyr.astype(F32)]
    convert_element_type x5 -> x1, other arithmetic: 13.5 us -> 0.74 us  [split_router(): wrt = jnp.concatenate([pad(hi), pad(hi), pad(lo)], axis=1).T.astype(BF)]
  transfers between devices with their start and end apart: 8 -> 4, of which waited for: 0 -> 0; matrix products, arithmetic and copies ran while one was open for 24% -> 32% of each run, Pallas kernels for 0% -> 41%
where the time goes in v2:
time: 720 us; the launch traced here: 719 us
  Pallas kernels  435 us (60%)
  local copies, waits for them, and re-layouts  173 us (24%)
  other arithmetic  41.2 us (6%)
  blocking collectives  40.3 us (6%)
  matrix products  18 us (2%)
    pallas_call x2, Pallas kernels, expert_call(): pl.pallas_call(functools.partial(expert_kernel, cfg), out_shape=out_shape...  435 us
    gather x4, local copies, waits for them, and re-layouts, gather_rows(): return jnp.take(source, row_index, axis=0, mode='fill', fill_value=0)  97 us
    psum x1, blocking collectives, expert_layer(): fin = lax.psum(fin, 'ep')  40.3 us
    gather x1, local copies, waits for them, and re-layouts, expert_layer(): jnp.take(back, jnp.minimum(tok_slot, n_slots - 1), axis=0, mode='clip')  36.8 us
    scatter x1, local copies, waits for them, and re-layouts, expert_layer(): jnp.full((n_slots,), tokens, jnp.int32).at[tok_slot]  30.5 us
  transfers between devices with their start and end apart: 4, of which 0 were waited for; matrix products, arithmetic and copies ran while one was open for 32% of the time, Pallas kernels for 41%

profile of v2, /device:TPU:0, one launch (start us, length us, event | category | flops | bytes accessed | tf_op | source)
XLA Modules:
  0.0 718.9 jit_solution(10284200380419791505)
XLA Ops:
  0.6 4.2 collective-permute-start
  4.9 0.9 fusion.4
  5.8 9.5 %reduce-window.6 = s32[32,64,128]{2,1,0:T(8,128)S(1)} reduce-window(s32[32,64,128]{2,1,0:T(8,128)S(1)} %fusion.4, s32[]{:T(128)} %constant.68.clone.1), window={size=1x1x128 pad=0_0x0_0x127_0}, to_apply=%region_0.1 | reduce-window | flops 33292288 | bytes 2097156 | tf_op jit(solution)/shard_map/reduce-window
  15.3 0.9 slice_reduce_fusion
  18.3 30.5 %scatter_custom_fusion = s32[10240]{0:T(1024)S(1)} fusion(s32[8192]{0:T(1024)S(1)} %get-tuple-element.41, s32[8192]{0:T(1024)S(1)} %iota.11, s32[]{:T(128)} %constant.72.clone.1), kind=kCustom, calls=%fused_computation.62 | custom fusion | bytes 40964 | tf_op jit(solution)/shard_map/scatter | solution.py:314
  48.8 24.3 %gather_fusion.1 = bf16[5120,384]{1,0:T(8,128)(2,1)} fusion(bf16[8192,384]{1,0:T(8,128)(2,1)} %param.8, s32[5120]{0:T(1024)S(1)} %get-tuple-element.47), kind=kCustom, calls=%fused_computation.clone | custom fusion | bytes 7884800 | tf_op jit(solution)/shard_map/jit(_take)/gather | solution.py:19
  73.1 24.2 %gather_fusion.2 = bf16[5120,384]{1,0:T(8,128)(2,1)} fusion(bf16[8192,384]{1,0:T(8,128)(2,1)} %param.13, s32[5120]{0:T(1024)S(1)} %get-tuple-element.47), kind=kCustom, calls=%fused_computation.1.clone | custom fusion | bytes 7884800 | tf_op jit(solution)/shard_map/jit(_take)/gather | solution.py:19
  97.3 24.2 %gather_fusion.3 = bf16[5120,384]{1,0:T(8,128)(2,1)} fusion(bf16[8192,384]{1,0:T(8,128)(2,1)} %param.8, s32[5120]{0:T(1024)S(1)} %get-tuple-element.46), kind=kCustom, calls=%fused_computation.2.clone | custom fusion | bytes 7884800 | tf_op jit(solution)/shard_map/jit(_take)/gather | solution.py:19
  121.5 24.3 %gather_fusion.4 = bf16[5120,384]{1,0:T(8,128)(2,1)} fusion(bf16[8192,384]{1,0:T(8,128)(2,1)} %param.13, s32[5120]{0:T(1024)S(1)} %get-tuple-element.46), kind=kCustom, calls=%fused_computation.3.clone | custom fusion | bytes 7884800 | tf_op jit(solution)/shard_map/jit(_take)/gather | solution.py:19
  146.7 4.8 fusion.33
  152.6 11.9 %broadcast_select_fusion = (bf16[5120,384]{1,0:T(8,128)(2,1)}, bf16[5120,384]{1,0:T(8,128)(2,1)}, bf16[5120,384]{1,0:T(8,128)(2,1)}, bf16[5120,384]{1,0:T(8,128)(2,1)}) fusion(bf16[5120,384]{1,0:T(8,128)(2,1)} %gather_fusion.4, pred[5120]{0:T(1024)(128)(4,1)S(1)} %get-tuple-element.44, bf16[5120,384]{1,0:T(8,128)(2,1)} %gather_fusion.3, ...), kind=kLoop, calls=%fused_computation.9 | loop fusion | flops 7864320 | bytes 31467520 | tf_op jit(solution)/shard_map/jit(_take)/select_n | solution.py:19
  165.5 139.0 %expert_a.1 = (bf16[16,320,384]{2,1,0:T(8,128)(2,1)}, f32[384,1536]{1,0:T(8,128)}, f32[1536,384]{1,0:T(8,128)}, f32[384,128]{1,0:T(8,128)}, f32[8,128]{1,0:T(8,128)}) custom-call(f32[8,128]{1,0:T(8,128)} %broadcast_in_dim.73.refs_0_, bf16[16,320,384]{2,1,0:T(8,128)(2,1)} %bitcast.48, bf16[16,320,384]{2,1,0:T(8,128)(2,1)} %bitcast.49, ...), custom_call_target="tpu_custom_call" | custom-call | flops 36238786560 | bytes 33554432 | tf_op jit(solution)/shard_map/expert_a/pallas_call | solution.py:273
  305.2 2.8 collective-permute-start.3
  308.2 296.3 %expert_b.1 = (bf16[16,320,384]{2,1,0:T(8,128)(2,1)}, bf16[16,320,384]{2,1,0:T(8,128)(2,1)}, f32[384,1536]{1,0:T(8,128)}, f32[1536,384]{1,0:T(8,128)}, f32[384,128]{1,0:T(8,128)}) custom-call(f32[8,128]{1,0:T(8,128)} %get-tuple-element.17.refs_0_, bf16[16,320,384]{2,1,0:T(8,128)(2,1)} %get-tuple-element.18.refs_1_, bf16[16,320,384]{2,1,0:T(8,128)(2,1)} %bitcast.47, ...), custom_call_target="tpu_custom_call" | custom-call | flops 36238786560 | bytes 33554432 | tf_op jit(solution)/shard_map/expert_b/pallas_call | solution.py:273
  606.3 5.5 fusion.15
  611.9 1.0 reshape.84
  613.6 40.3 %psum.7 = f32[12321]{0:T(1024)S(1)} all-reduce(f32[12321]{0:T(1024)S(1)} %concatenate.17), channel_id=1, replica_groups=mesh['ep'=32] {'ep'}, use_global_device_ids=true, to_apply=%region_11.13 | all-reduce | flops 12321 | bytes 98568 | tf_op jit(solution)/shard_map/psum | solution.py:343
  655.3 1.7 copy.18
  657.0 1.3 fusion.25
  659.6 7.3 %pad_maximum_fusion = bf16[32,320,384]{2,1,0:T(8,128)(2,1)} fusion(bf16[16,320,384]{2,1,0:T(8,128)(2,1)} %get-tuple-element.20, bf16[16,320,384]{2,1,0:T(8,128)(2,1)} %get-tuple-element.19), kind=kLoop, calls=%fused_computation.8 | loop fusion | flops 3932160 | bytes 15728640 | tf_op jit(solution)/shard_map/concatenate | solution.py:339
  666.9 36.8 %gather_fusion = bf16[8192,384]{1,0:T(8,128)(2,1)} fusion(bf16[10240,384]{1,0:T(8,128)(2,1)} %bitcast.44, s32[8192]{0:T(1024)S(1)} %copy-done.5), kind=kCustom, calls=%fused_computation.4 | custom fusion | bytes 12615680 | tf_op jit(solution)/shard_map/jit(_take)/gather | solution.py:340
  703.7 7.6 %fusion = bf16[8192,384]{1,0:T(8,128)(2,1)} fusion(bf16[8192,384]{1,0:T(8,128)(2,1)} %gather_fusion, f32[384,32]{0,1:T(8,128)S(1)} %copy-done.4, pred[8192]{0:T(1024)(128)(4,1)} %copy-done.10, f32[8192]{0:T(1024)} %copy-done.9, f32[8192]{0:T(1024)} %copy-done.8, f32[32]{0:T(128)} %copy-done.11, f32[8192,32]{0,1:T(8,128)S(1)} %get-tuple-element.53, ...), kind=kOutput, calls=%fused_computation.7 | convolution fusion | flops 205783040 | bytes 13820032 | tf_op jit(solution)/shard_map/te,de->td/dot_general | solution.py:337
  711.3 3.5 add_bitcast_fusion
  714.8 1.8 add_bitcast_fusion.1
  (59 shorter events, 9.8 us)
Async XLA Ops:
  0.6 16.1 %copy-start.2 = (s32[8192]{0:T(1024)S(1)}, s32[8192]{0:T(1024)}, u32[]{:S(2)}) copy-start(s32[8192]{0:T(1024)} %param.10) | copy-start | bytes 98308
  0.6 163.9 %collective-permute-start = (bf16[384,1536]{1,0:T(8,128)(2,1)}, bf16[384,1536]{1,0:T(8,128)(2,1)S(1)}, u32[]{:S(2)}, u32[]{:S(2)}) collective-permute-start(bf16[384,1536]{1,0:T(8,128)(2,1)} %bitcast.52), channel_id=1, source_target_pairs={{0,16},{1,17},{2,18},{3,19},{4,20},{5,21},{6,22},{7,23},{8,24},{9,... | collective-permute-start | bytes 3538952 | tf_op jit(solution)/shard_map/ppermute | solution.py:305
  4.8 159.7 %collective-permute-start.1 = (bf16[1536,384]{1,0:T(8,128)(2,1)}, bf16[1536,384]{1,0:T(8,128)(2,1)}, u32[]{:S(2)}, u32[]{:S(2)}) collective-permute-start(bf16[1536,384]{1,0:T(8,128)(2,1)} %bitcast.54), channel_id=1, source_target_pairs={{0,16},{1,17},{2,18},{3,19},{4,20},{5,21},{6,22},{7,23},{8,24},{9,... | collective-permute-start | bytes 3538952 | tf_op jit(solution)/shard_map/ppermute | solution.py:306
  121.5 24.4 %copy-start.3 = (f32[384,32]{0,1:T(8,128)S(1)}, f32[384,32]{0,1:T(8,128)}, u32[]{:S(2)}) copy-start(f32[384,32]{0,1:T(8,128)} %param.9) | copy-start | bytes 147460
  151.5 454.2 %copy-start.10 = (pred[8192]{0:T(1024)(128)(4,1)}, pred[8192]{0:T(1024)(128)(4,1)S(1)}, u32[]{:S(2)}) copy-start(pred[8192]{0:T(1024)(128)(4,1)S(1)} %add_compare_fusion) | copy-start | bytes 24580
  152.6 453.1 %copy-start.6 = (f32[8192]{0:T(1024)}, f32[8192]{0:T(1024)S(1)}, u32[]{:S(2)}) copy-start(f32[8192]{0:T(1024)S(1)} %fusion.6) | copy-start | bytes 98308
  164.5 1.0 copy-start.12
  305.2 300.5 %copy-start.11 = (f32[32]{0:T(128)}, f32[32]{0:T(128)S(1)}, u32[]{:S(2)}) copy-start(f32[32]{0:T(128)S(1)} %multiply_bitcast_fusion) | copy-start | bytes 388
  305.2 406.1 %collective-permute-start.3 = (f32[1536,384]{1,0:T(8,128)}, f32[1536,384]{1,0:T(8,128)}, u32[]{:S(2)}, u32[]{:S(2)}) collective-permute-start(f32[1536,384]{1,0:T(8,128)} %get-tuple-element.24), channel_id=1, source_target_pairs={{0,16},{1,17},{2,18},{3,19},{4,20},{5,21},{6,22},{7,23},{8,24},{9,... | collective-permute-start | bytes 7077896 | tf_op jit(solution)/shard_map/ppermute | solution.py:325
  308.1 406.8 %collective-permute-start.2 = (f32[384,1536]{1,0:T(8,128)}, f32[384,1536]{1,0:T(8,128)S(1)}, u32[]{:S(2)}, u32[]{:S(2)}) collective-permute-start(f32[384,1536]{1,0:T(8,128)} %get-tuple-element.22), channel_id=1, source_target_pairs={{0,16},{1,17},{2,18},{3,19},{4,20},{5,21},{6,22},{7,23},{8,24},{9,... | collective-permute-start | bytes 7077896 | tf_op jit(solution)/shard_map/ppermute | solution.py:324
  308.2 298.2 %copy-start.13 = (f32[384,128]{1,0:T(8,128)S(1)}, f32[384,128]{1,0:T(8,128)}, u32[]{:S(2)}) copy-start(f32[384,128]{1,0:T(8,128)} %get-tuple-element.25) | copy-start | bytes 589828
  605.1 0.6 copy-start.8
  605.7 0.6 copy-start.9
  659.6 7.3 %copy-start.5 = (s32[8192]{0:T(1024)S(1)}, s32[8192]{0:T(1024)}, u32[]{:S(2)}) copy-start(s32[8192]{0:T(1024)} %get-tuple-element.40) | copy-start | bytes 98308
  666.9 36.8 %copy-start.4 = (f32[384,32]{0,1:T(8,128)S(1)}, f32[384,32]{0,1:T(8,128)}, u32[]{:S(2)}) copy-start(f32[384,32]{0,1:T(8,128)} %param.9) | copy-start | bytes 147460
  666.9 36.8 %copy-start.7 = (f32[8192]{0:T(1024)S(1)}, f32[8192]{0:T(1024)}, u32[]{:S(2)}) copy-start(f32[8192]{0:T(1024)} %copy-done.6) | copy-start | bytes 98308
  703.7 7.6 %copy-start.1 = (f32[1536,384]{1,0:T(8,128)S(1)}, f32[1536,384]{1,0:T(8,128)}, u32[]{:S(2)}) copy-start(f32[1536,384]{1,0:T(8,128)} %get-tuple-element.23) | copy-start | bytes 7077892
  711.3 3.5 copy-start

commit v3 on v2

v3 whole, which is shorter than its diff:
```python
import functools
import jax
import jax.numpy as jnp
from jax import lax
from jax.experimental import pallas as pl
from jax.experimental.pallas import tpu as pltpu
from jax.sharding import PartitionSpec as P

AUX_WEIGHT = 0.01
Z_WEIGHT = 0.001
BF = jnp.bfloat16
F32 = jnp.float32
LANES = 128
MESH_ID = pl.DeviceIdType.MESH
VMEM_LIMIT = 60 * 1024 * 1024
VM = pl.BlockSpec(memory_space=pltpu.VMEM)
SM = pl.BlockSpec(memory_space=pltpu.SMEM)
HBM = pl.BlockSpec(memory_space=pltpu.HBM)


def xor3(a, b):
    out = 0
    for k in (1, 2, 4):
        out = out + k * lax.rem(a // k + b // k, 2)
    return out


def dot(a, b, ca=1, cb=0):
    return lax.dot_general(a, b, (((ca,), (cb,)), ((), ())), preferred_element_type=F32)


def expert_kernel(cfg, *refs):
    n_dev, hd, cap, d, ff, ft, total_tok, first = cfg
    lead, sx, sdy, wi, wo, wr, wrt, gx_out, gwi, gwo, gwr = refs[:11]
    rest = refs[11:]
    if first:
        tot_ref, cbuf, csend, crecv = rest[0], *rest[1:4]
        rest = rest[4:]
    xr, dyr, gwot, dlw, oacc, dracc, gb, xt, gt, stage, loc_sem, send_sem, recv_sem, out_sem = rest
    me = lax.axis_index('ep')
    half = me // hd
    rank = lax.rem(me, hd)
    chip = rank // 2
    core = lax.rem(rank, 2)
    n_grp = hd // 2
    rows = 2 * cap
    off = 0 if first else hd

    def peer_of(j, c):
        return xor3(chip, j) * 2 + lax.rem(core + c, 2)

    def token_copy(a, src, dst, peer, slot):
        return pltpu.make_async_remote_copy(
            src_ref=src.at[off + peer], dst_ref=dst.at[slot], send_sem=send_sem.at[a, peer],
            recv_sem=recv_sem.at[a, slot], device_id=(half * hd + peer,), device_id_type=MESH_ID)

    if first:
        def count_copy(k, sending):
            peer = lax.rem(me + k, n_dev)
            slot = me if sending else peer
            return pltpu.make_async_remote_copy(
                src_ref=lead, dst_ref=cbuf.at[slot], send_sem=csend.at[peer],
                recv_sem=crecv.at[slot], device_id=(peer,), device_id_type=MESH_ID)

        def start_count(k, _):
            count_copy(k, True).start()
            return 0
        lax.fori_loop(1, n_dev, start_count, 0)
        cbuf[me] = lead[...]

    own_x = pltpu.make_async_copy(sx.at[off + rank], xr.at[rank], loc_sem.at[0])
    own_dy = pltpu.make_async_copy(sdy.at[off + rank], dyr.at[rank], loc_sem.at[1])
    own_x.start()
    own_dy.start()

    def start_peer(peer):
        token_copy(0, sx, xr, peer, rank).start()
        token_copy(1, sdy, dyr, peer, rank).start()

    start_peer(peer_of(0, 1))

    def start_group(j, _):
        start_peer(peer_of(j, 0))
        start_peer(peer_of(j, 1))
        return 0
    lax.fori_loop(1, n_grp, start_group, 0)

    gwi[...] = jnp.zeros_like(gwi)
    gwot[...] = jnp.zeros_like(gwot)
    gwr[...] = jnp.zeros_like(gwr)

    if first:
        def wait_count(k, _):
            count_copy(k, False).wait_recv()
            return 0
        lax.fori_loop(1, n_dev, wait_count, 0)
        tot_ref[...] = jnp.sum(cbuf[...], axis=0)
        tot = tot_ref[0:1, :]
        e_id = me
    else:
        tot = lead[0:1, :]
        e_id = lax.rem(me + hd, n_dev)
    v = tot * (AUX_WEIGHT * n_dev / (float(total_tok) * total_tok))
    zc = 2.0 * Z_WEIGHT / total_tok

    def recv_wait(peer):
        token_copy(0, sx, xr, peer, peer).wait_recv()
        token_copy(1, sdy, dyr, peer, peer).wait_recv()

    def group(j, _):
        @pl.when(j == 0)
        def _():
            own_x.wait()
            own_dy.wait()

        @pl.when(j > 0)
        def _():
            recv_wait(peer_of(j, 0))
        recv_wait(peer_of(j, 1))
        pair = xor3(chip, j)
        x = xr[pl.ds(2 * pair, 2)].reshape(rows, d)
        dyf = dyr[pl.ds(2 * pair, 2)].reshape(rows, d).astype(F32)
        lane = lax.broadcasted_iota(jnp.int32, (rows, LANES), 1)
        p, lz = router_rows(x, wr, lane, n_dev)
        hot = (lane == e_id).astype(F32)
        gate = jnp.sum(p * hot, axis=1, keepdims=True)
        g = (gate * dyf).astype(BF)
        gb[...] = g
        xt[...] = x.T
        gt[...] = g.T
        oacc[...] = jnp.zeros_like(oacc)
        dracc[...] = jnp.zeros_like(dracc)

        def ff_tile(f, _):
            fo = pl.multiple_of(f * ft, ft)
            wit = wi[:, pl.ds(fo, ft)]
            wot = wo[pl.ds(fo, ft), :]
            xx = xr[pl.ds(2 * pair, 2)].reshape(rows, d)
            h = jnp.maximum(dot(xx, wit), 0.0).astype(BF)
            oacc[...] += dot(h, wot)
            dh = dot(gb[...], wot, 1, 1)
            da = jnp.where(h > 0, dh, 0.0).astype(BF)
            dracc[...] += dot(da, wit, 1, 1)
            gwot[:, pl.ds(fo, ft)] += dot(gt[...], h)
            gwi[:, pl.ds(fo, ft)] += dot(xt[...], da)
            return 0
        lax.fori_loop(0, ff // ft, ff_tile, 0)

        o = oacc[...].astype(BF).astype(F32)
        dgate = jnp.sum(o * dyf, axis=1, keepdims=True)
        dl = (gate * dgate) * (hot - p) + base_grad(p, lz, v, zc)
        dl2, dl3 = split_rows(dl)
        dlw[...] = dot(dl3, wrt[...])
        gw = dot(xt[...], dl2)
        gwr[...] += gw[:, :LANES] + gw[:, LANES:]
        gx = (dracc[...].astype(BF).astype(F32) + dlw[...]).astype(BF)
        stage[pl.ds(2 * pair, 2)] = gx.reshape(2, cap, d)
        pltpu.make_async_copy(stage.at[pl.ds(2 * pair, 2)], gx_out.at[pl.ds(2 * pair, 2)], out_sem.at[pair]).start()
        return 0
    lax.fori_loop(0, n_grp, group, 0)

    def finish(f, _):
        fo = pl.multiple_of(f * ft, ft)
        gwo[pl.ds(fo, ft), :] = gwot[:, pl.ds(fo, ft)].T
        return 0
    lax.fori_loop(0, ff // ft, finish, 0)

    def send_wait(peer):
        token_copy(0, sx, xr, peer, peer).wait_send()
        token_copy(1, sdy, dyr, peer, peer).wait_send()

    send_wait(peer_of(0, 1))

    def drain(j, _):
        send_wait(peer_of(j, 0))
        send_wait(peer_of(j, 1))
        return 0
    lax.fori_loop(1, n_grp, drain, 0)

    def out_wait(s, _):
        pltpu.make_async_copy(stage.at[pl.ds(2 * s, 2)], gx_out.at[pl.ds(2 * s, 2)], out_sem.at[s]).wait()
        return 0
    lax.fori_loop(0, n_grp, out_wait, 0)
    if first:
        def count_drain(k, _):
            count_copy(k, False).wait_send()
            return 0
        lax.fori_loop(1, n_dev, count_drain, 0)


def router_rows(x, wr, lane, n_dev):
    lg = dot(x, wr[...])
    lg = jnp.where(lane < n_dev, lg[:, :LANES] + lg[:, LANES:], -1e30)
    mx = jnp.max(lg, axis=1, keepdims=True)
    ex = jnp.exp(lg - mx)
    sm = jnp.sum(ex, axis=1, keepdims=True)
    return ex / sm, mx + jnp.log(sm)


def base_grad(p, lz, v, zc):
    spread = jnp.sum(p * v, axis=1, keepdims=True)
    return p * (v - spread) + (zc * lz) * p


def split_rows(dl):
    hi = dl.astype(BF)
    lo = (dl - hi.astype(F32)).astype(BF)
    dl2 = jnp.concatenate([hi, lo], axis=1)
    return dl2, jnp.concatenate([dl2, hi], axis=1)


def expert_call(cfg, *args):
    n_dev, hd, cap, d, ff, ft, total_tok, first = cfg
    sd = jax.ShapeDtypeStruct
    rows = 2 * cap
    dma = pltpu.SemaphoreType.DMA
    scratch = [pltpu.VMEM((hd, cap, d), BF), pltpu.VMEM((hd, cap, d), BF), pltpu.VMEM((d, ff), F32),
               pltpu.VMEM((rows, d), F32), pltpu.VMEM((rows, d), F32), pltpu.VMEM((rows, d), F32),
               pltpu.VMEM((rows, d), BF), pltpu.VMEM((d, rows), BF), pltpu.VMEM((d, rows), BF),
               pltpu.VMEM((hd, cap, d), BF), dma((2,)), dma((2, hd)), dma((2, hd)), dma((hd // 2,))]
    out_shape = [sd((hd, cap, d), BF), sd((d, ff), F32), sd((ff, d), F32), sd((d, LANES), F32)]
    out_specs = [HBM, VM, VM, VM]
    if first:
        out_shape.append(sd((8, LANES), F32))
        out_specs.append(VM)
        scratch = [pltpu.VMEM((n_dev, 8, LANES), F32), dma((n_dev,)), dma((n_dev,))] + scratch
    return pl.pallas_call(
        functools.partial(expert_kernel, cfg), out_shape=out_shape, in_specs=[VM, HBM, HBM, VM, VM, VM, VM],
        out_specs=out_specs, scratch_shapes=scratch, name='expert_own' if first else 'expert_mirror',
        cost_estimate=pl.CostEstimate(flops=12 * hd * cap * d * ff, bytes_accessed=32 * 2 ** 20, transcendentals=0),
        compiler_params=pltpu.CompilerParams(has_side_effects=True, vmem_limit_bytes=VMEM_LIMIT))(*args)


def return_kernel(hd, go, gm, bo, bm, loc_sem, send_sem, recv_sem):
    me = lax.axis_index('ep')
    half = me // hd
    rank = lax.rem(me, hd)
    chip = rank // 2
    core = lax.rem(rank, 2)

    def peer_of(j, c):
        return xor3(chip, j) * 2 + lax.rem(core + c, 2)

    def row_copy(a, peer, slot):
        src, dst = ((go, bo), (gm, bm))[a]
        return pltpu.make_async_remote_copy(
            src_ref=src.at[peer], dst_ref=dst.at[slot], send_sem=send_sem.at[a, peer],
            recv_sem=recv_sem.at[a, slot], device_id=(half * hd + peer,), device_id_type=MESH_ID)

    own = [pltpu.make_async_copy(s.at[rank], t.at[rank], loc_sem.at[a]) for a, (s, t) in enumerate(((go, bo), (gm, bm)))]

    def start(peer):
        for a in (0, 1):
            row_copy(a, peer, rank).start()

    def wait(peer):
        for a in (0, 1):
            row_copy(a, peer, peer).wait_send()
            row_copy(a, peer, peer).wait_recv()

    def each(fn):
        fn(peer_of(0, 1))

        def body(j, _):
            fn(peer_of(j, 0))
            fn(peer_of(j, 1))
            return 0
        lax.fori_loop(1, hd // 2, body, 0)
    each(start)
    for c in own:
        c.start()
    for c in own:
        c.wait()
    each(wait)


def return_call(go, gm):
    hd = go.shape[0]
    dma = pltpu.SemaphoreType.DMA
    sd = jax.ShapeDtypeStruct(go.shape, BF)
    return pl.pallas_call(
        functools.partial(return_kernel, hd), out_shape=[sd, sd], in_specs=[HBM, HBM], out_specs=[HBM, HBM],
        scratch_shapes=[dma((2,)), dma((2, hd)), dma((2, hd))], name='row_return',
        cost_estimate=pl.CostEstimate(flops=10 ** 10, bytes_accessed=32 * 2 ** 20, transcendentals=0),
        compiler_params=pltpu.CompilerParams(has_side_effects=True))(go, gm)


def route_kernel(ne, cap, half_ref, idx_ref, slot_ref, cnt_ref, hot, cum):
    nb = idx_ref.shape[0]
    expert = lax.broadcasted_iota(jnp.int32, (ne, LANES), 0)
    shift = half_ref[0] * (ne // 2)
    for b in range(nb):
        hot[b * ne:(b + 1) * ne, :] = (expert == idx_ref[b:b + 1, :]).astype(F32)
    r = lax.broadcasted_iota(jnp.int32, (LANES, 2 * LANES), 0)
    c = lax.broadcasted_iota(jnp.int32, (LANES, 2 * LANES), 1)
    tri = ((r <= c) | (c >= LANES)).astype(F32).astype(BF)
    cum[...] = dot(hot[...].astype(BF), tri)
    carry = jnp.zeros((ne, LANES), F32)
    for b in range(nb):
        block = cum[b * ne:(b + 1) * ne, :]
        pos = jnp.sum(hot[b * ne:(b + 1) * ne, :] * (block[:, :LANES] + carry), axis=0, keepdims=True) - 1.0
        pos = pos.astype(jnp.int32)
        rel = idx_ref[b:b + 1, :] + shift
        rel = jnp.where(rel >= ne, rel - ne, rel)
        slot_ref[b:b + 1, :] = jnp.where(pos < cap, rel * cap + pos, ne * cap)
        carry = carry + block[:, LANES:]
    full = jnp.concatenate([carry, jnp.zeros((LANES - ne, LANES), F32)], axis=0)
    cnt_ref[...] = full.T[0:8, :]


def route_call(half, idx, ne, cap):
    nb = idx.shape[0] // LANES
    sd = jax.ShapeDtypeStruct
    return pl.pallas_call(
        functools.partial(route_kernel, ne, cap), out_shape=[sd((nb, LANES), jnp.int32), sd((8, LANES), F32)],
        in_specs=[SM, VM], out_specs=[VM, VM],
        scratch_shapes=[pltpu.VMEM((nb * ne, LANES), F32), pltpu.VMEM((nb * ne, 2 * LANES), F32)], name='route',
        compiler_params=pltpu.CompilerParams(vmem_limit_bytes=VMEM_LIMIT))(half, idx.reshape(nb, LANES))


def dispatch_kernel(nb, tb, ne, cap, d, slot_ref, cnt_ref, x_ref, dy_ref, sx_ref, sdy_ref, tmp, big):
    i = pl.program_id(0)
    nk = d // LANES

    @pl.when(i < nb)
    def _():
        xf = x_ref[...].astype(F32)
        df = dy_ref[...].astype(F32)
        for k in range(nk):
            tmp[pl.ds(k, tb, stride=8), :] = xf[:, k * LANES:(k + 1) * LANES]
            tmp[pl.ds(4 + k, tb, stride=8), :] = df[:, k * LANES:(k + 1) * LANES]

        def place(q, _):
            row = i * (tb // LANES) + q // (LANES // 16)
            col = lax.rem(q, LANES // 16) * 16
            for u in range(16):
                s = slot_ref[row, col + u]
                big[pl.ds(pl.multiple_of(s * 8, 8), 8), :] = tmp[pl.ds(pl.multiple_of((q * 16 + u) * 8, 8), 8), :]
            return 0
        lax.fori_loop(0, tb // 16, place, 0)

    @pl.when(i >= nb)
    def _():
        e = i - nb
        n = cnt_ref[e]
        ok = lax.broadcasted_iota(jnp.int32, (cap, LANES), 0) < n
        base = e * (cap * 8)
        for k in range(nk):
            xk = big[pl.ds(base + k, cap, stride=8), :]
            sx_ref[0, :, k * LANES:(k + 1) * LANES] = jnp.where(ok, xk, 0.0).astype(BF)
            dk = big[pl.ds(base + 4 + k, cap, stride=8), :]
            sdy_ref[0, :, k * LANES:(k + 1) * LANES] = jnp.where(ok, dk, 0.0).astype(BF)


def dispatch_call(slot, cnt, x, dy, ne, cap):
    t, d = x.shape
    tb = 512
    nb = t // tb
    sd = jax.ShapeDtypeStruct((ne, cap, d), BF)
    tok = pl.BlockSpec((tb, d), lambda i: (jnp.minimum(i, nb - 1), 0))
    out = pl.BlockSpec((1, cap, d), lambda i: (jnp.maximum(i - nb, 0), 0, 0))
    return pl.pallas_call(
        functools.partial(dispatch_kernel, nb, tb, ne, cap, d), grid=(nb + ne,), out_shape=[sd, sd],
        in_specs=[SM, SM, tok, tok], out_specs=[out, out],
        scratch_shapes=[pltpu.VMEM((tb * 8, LANES), F32), pltpu.VMEM((ne * cap * 8 + 8, LANES), F32)], name='dispatch',
        compiler_params=pltpu.CompilerParams(vmem_limit_bytes=VMEM_LIMIT))(slot, cnt, x, dy)


def combine_kernel(cfg, slot_ref, tot_ref, bo, bm, x_ref, wr, wrt, gx_ref, gwr, stat, tmp, big):
    nb, tb, n_dev, hd, cap, d, total_tok = cfg
    i = pl.program_id(0)
    nk = d // LANES

    def put(rows, e):
        f = rows.astype(F32)
        base = e * (cap * 8)
        for k in range(nk):
            big[pl.ds(base + k, cap, stride=8), :] = f[:, k * LANES:(k + 1) * LANES]
        big[pl.ds(base + nk, cap, stride=8), :] = jnp.zeros((cap, LANES), F32)

    @pl.when(i == 0)
    def _():
        big[n_dev * cap * 8:n_dev * cap * 8 + 8, :] = jnp.ones((8, LANES), F32)
        gwr[...] = jnp.zeros_like(gwr)
        stat[...] = jnp.zeros_like(stat)

    @pl.when(i < hd)
    def _():
        put(bo[0], i)

    @pl.when((i >= hd) & (i < n_dev))
    def _():
        put(bm[0], i)

    @pl.when(i >= n_dev)
    def _():
        b = i - n_dev

        def fetch(q, _):
            row = b * (tb // LANES) + q // (LANES // 16)
            col = lax.rem(q, LANES // 16) * 16
            for u in range(16):
                s = slot_ref[row, col + u]
                tmp[pl.ds(pl.multiple_of((q * 16 + u) * 8, 8), 8), :] = big[pl.ds(pl.multiple_of(s * 8, 8), 8), :]
            return 0
        lax.fori_loop(0, tb // 16, fetch, 0)
        x = x_ref[...]
        lane = lax.broadcasted_iota(jnp.int32, (tb, LANES), 1)
        p, lz = router_rows(x, wr, lane, n_dev)
        v = tot_ref[0:1, :] * (AUX_WEIGHT * n_dev / (float(total_tok) * total_tok))
        dl = base_grad(p, lz, v, 2.0 * Z_WEIGHT / total_tok)
        _, dl3 = split_rows(dl)
        gxd = dot(dl3, wrt[...])
        drop = tmp[pl.ds(nk, tb, stride=8), :]
        dl2, _ = split_rows(dl * drop)
        gw = lax.dot_general(x, dl2, (((0,), (0,)), ((), ())), preferred_element_type=F32)
        gwr[...] += gw[:, :LANES] + gw[:, LANES:]
        stat[0:1, :] += jnp.sum(p, axis=0, keepdims=True)
        stat[1:2, :] += jnp.sum(jnp.broadcast_to(lz * lz, (tb, LANES)), axis=0, keepdims=True)
        for k in range(nk):
            got = tmp[pl.ds(k, tb, stride=8), :]
            gx_ref[:, k * LANES:(k + 1) * LANES] = jnp.where(drop > 0.5, gxd[:, k * LANES:(k + 1) * LANES], got).astype(BF)


def combine_call(slot, tot, bo, bm, x, wr, wrt, total_tok):
    t, d = x.shape
    hd, cap, _ = bo.shape
    n_dev = 2 * hd
    tb = 512
    nb = t // tb
    sd = jax.ShapeDtypeStruct
    tok = pl.BlockSpec((tb, d), lambda i: (jnp.maximum(i - n_dev, 0), 0))
    const = lambda s: pl.BlockSpec(s, lambda i: (0, 0))
    return pl.pallas_call(
        functools.partial(combine_kernel, (nb, tb, n_dev, hd, cap, d, total_tok)), grid=(n_dev + nb,),
        out_shape=[sd((t, d), BF), sd((d, LANES), F32), sd((8, LANES), F32)],
        in_specs=[SM, VM, pl.BlockSpec((1, cap, d), lambda i: (jnp.minimum(i, hd - 1), 0, 0)),
                  pl.BlockSpec((1, cap, d), lambda i: (jnp.clip(i - hd, 0, hd - 1), 0, 0)), tok, VM, VM],
        out_specs=[tok, const((d, LANES)), const((8, LANES))],
        scratch_shapes=[pltpu.VMEM((tb * 8, LANES), F32), pltpu.VMEM((n_dev * cap * 8 + 8, LANES), F32)], name='combine',
        compiler_params=pltpu.CompilerParams(vmem_limit_bytes=VMEM_LIMIT))(slot, tot, bo, bm, x, wr, wrt)


def split_router(w_router):
    d, ne = w_router.shape
    hi = lax.reduce_precision(w_router, 8, 7)
    lo = lax.reduce_precision(w_router - hi, 8, 7)
    pad = lambda a: jnp.pad(a, ((0, 0), (0, LANES - ne)))
    wr = jnp.concatenate([pad(hi), pad(lo)], axis=1).astype(BF)
    wrt = jnp.concatenate([pad(hi), pad(hi), pad(lo)], axis=1).T.astype(BF)
    return wr, wrt


def solution(mesh):
    n_dev = mesh.shape['ep']
    hd = n_dev // 2
    mirror = [(i, (i + hd) % n_dev) for i in range(n_dev)]

    def expert_layer(x_tokens, w_router, expert_idx, w_in, w_out, grad_y):
        tokens, d_model = x_tokens.shape
        ff = w_in.shape[-1]
        ne = n_dev
        capacity = (5 * tokens + 4 * ne - 1) // (4 * ne)
        total_tok = tokens * n_dev
        me = lax.axis_index('ep')
        half = me // hd
        w_in_o, w_out_o = w_in[0], w_out[0]
        w_in_m = lax.ppermute(w_in_o, 'ep', mirror)
        w_out_m = lax.ppermute(w_out_o, 'ep', mirror)
        wr, wrt = split_router(w_router)

        slot, cnt = route_call(half.reshape(1).astype(jnp.int32), expert_idx, ne, capacity)
        own = cnt[0, :ne].astype(jnp.int32)
        rel_cnt = jnp.where(half == 0, own, jnp.roll(own, hd))
        sx, sdy = dispatch_call(slot, rel_cnt, x_tokens, grad_y, ne, capacity)
        base = (n_dev, hd, capacity, d_model, ff, 512, total_tok)
        gx_o, gwi_o, gwo_o, gwr_o, tot = expert_call(base + (True,), cnt, sx, sdy, w_in_o, w_out_o, wr, wrt)
        gx_m, gwi_m, gwo_m, gwr_m = expert_call(base + (False,), tot, sx, sdy, w_in_m, w_out_m, wr, wrt)
        gwi_r = lax.ppermute(gwi_m, 'ep', mirror)
        gwo_r = lax.ppermute(gwo_m, 'ep', mirror)
        back_o, back_m = return_call(gx_o, gx_m)
        grad_x, gwr_d, stat = combine_call(slot, tot, back_o, back_m, x_tokens, wr, wrt, total_tok)

        fin = jnp.concatenate([(gwr_d + gwr_m + gwr_o)[:, :ne].reshape(-1), stat[0, :ne], stat[1, :1]])
        fin = lax.psum(fin, 'ep')
        nr = d_model * ne
        grad_w_router = fin[:nr].reshape(d_model, ne)
        aux_loss = AUX_WEIGHT * ne * jnp.sum(tot[0, :ne] / total_tok * fin[nr:nr + ne] / total_tok)
        z_loss = Z_WEIGHT * fin[nr + ne] / total_tok
        return grad_x, (gwi_o + gwi_r)[None], (gwo_o + gwo_r)[None], grad_w_router, aux_loss, z_loss

    return jax.shard_map(expert_layer, mesh=mesh,
                         in_specs=(P('ep', None), P(None, None), P('ep'), P('ep', None, None), P('ep', None, None), P('ep', None)),
                         out_specs=(P('ep', None), P('ep', None, None), P('ep', None, None), P(None, None), P(), P()),
                         check_vma=False)
```

time: 720 us -> 702 us (0.975)
  Pallas kernels: 435 us -> 623 us
  local copies, waits for them, and re-layouts: 173 us -> 6.44 us
  other arithmetic: 41.2 us -> 12.8 us
  matrix products: 18 us -> 0 us
    pallas_call x0 -> x4, Pallas kernels: none -> 342 us  [the longest x1 223 us: return_call(): pl.pallas_call(functools.partial(return_kernel, hd), out_shape=[sd, sd],...]
    pallas_call x2, Pallas kernels: 435 us -> 281 us  [expert_call(): pl.pallas_call(functools.partial(expert_kernel, cfg), out_shape=out_shape...]
    gather x5 -> x0, local copies, waits for them, and re-layouts: 134 us -> none  [the longest x4 97 us: gather_rows(): return jnp.take(source, row_index, axis=0, mode='fill', fill_value=0)]
    scatter x1 -> x0, local copies, waits for them, and re-layouts: 30.5 us -> none  [expert_layer(): jnp.full((n_slots,), tokens, jnp.int32).at[tok_slot]]
    dot_general x3 -> x0, matrix products: 18 us -> none  [the longest x1 7.59 us: expert_layer(): gx_drop = jnp.einsum('te,de->td', dl, w_router).astype(BF)]
    select_n x2 -> x1, other arithmetic: 11.9 us -> 1.27 us  [expert_layer(): rel_cnt = jnp.where(half == 0, own, jnp.roll(own, hd))]
    another operation x3 -> x0, other arithmetic: 10.1 us -> none
    concatenate x1 -> x0, other arithmetic: 7.28 us -> none  [expert_layer(): back = jnp.concatenate([back_o, back_m], axis=0).reshape(n_slots, d_model)]
  transfers between devices with their start and end apart: 4 -> 4, of which waited for: 0 -> 0; matrix products, arithmetic and copies ran while one was open for 32% -> 2% of each run, Pallas kernels for 41% -> 70%
where the time goes in v3:
time: 702 us; the launch traced here: 700 us
  Pallas kernels  623 us (89%)
  blocking collectives  46.6 us (7%)
  other arithmetic  12.8 us (2%)
  starting transfers between devices  7.23 us (1%)
    pallas_call x2, Pallas kernels, expert_call(): pl.pallas_call(functools.partial(expert_kernel, cfg), out_shape=out_shape...  281 us
    pallas_call x1, Pallas kernels, return_call(): pl.pallas_call(functools.partial(return_kernel, hd), out_shape=[sd, sd],...  223 us
    pallas_call x1, Pallas kernels, combine_call(): pl.pallas_call(functools.partial(combine_kernel, (nb, tb, n_dev, hd, cap,...  67 us
    pallas_call x1, Pallas kernels, dispatch_call(): pl.pallas_call(functools.partial(dispatch_kernel, nb, tb, ne, cap, d), gr...  50.1 us
    psum x1, blocking collectives, expert_layer(): fin = lax.psum(fin, 'ep')  46.6 us
  transfers between devices with their start and end apart: 4, of which 0 were waited for; matrix products, arithmetic and copies ran while one was open for 2% of the time, Pallas kernels for 70%

profile of v3, /device:TPU:0, one launch (start us, length us, event | category | flops | bytes accessed | tf_op | source)
XLA Modules:
  0.0 700.2 jit_solution(17791104918054692508)
XLA Ops:
  0.6 4.2 collective-permute-start
  4.9 0.8 fusion.2
  5.7 0.7 maximum_bitcast_fusion.refs_6_.wrt
  6.5 2.0 route.1
  8.5 0.7 slice_convert_fusion
  9.2 0.8 copy.15.refs_5_.wr
  10.0 1.3 broadcast_select_fusion.cnt_ref
  11.3 50.1 %dispatch.1 = (bf16[32,320,384]{2,1,0:T(8,128)(2,1)}, bf16[32,320,384]{2,1,0:T(8,128)(2,1)}) custom-call(s32[64,128]{1,0:T(8,128)} %get-tuple-element.24.slot_ref, s32[32]{0:T(128)} %broadcast_select_fusion.cnt_ref, bf16[8192,384]{1,0:T(8,128)(2,1)} %x_ref.3, bf16[8192,384]{1,0:T(8,128)(2,1)} %dy_ref.1), custom_call_target="tpu_custom_call" | custom-call | tf_op jit(solution)/shard_map/dispatch/pallas_call | solution.py:362
  61.4 146.4 %expert_own.1 = (bf16[16,320,384]{2,1,0:T(8,128)(2,1)}, f32[384,1536]{1,0:T(8,128)}, f32[1536,384]{1,0:T(8,128)}, f32[384,128]{1,0:T(8,128)}, f32[8,128]{1,0:T(8,128)}) custom-call(f32[8,128]{1,0:T(8,128)} %get-tuple-element.25.refs_0_, bf16[32,320,384]{2,1,0:T(8,128)(2,1)} %get-tuple-element.26.refs_1_, bf16[32,320,384]{2,1,0:T(8,128)(2,1)} %get-tuple-element.27.refs_2_, ...), custom_call_target="tpu_custom_call" | custom-call | flops 36238786560 | bytes 33554432 | tf_op jit(solution)/shard_map/expert_own/pallas_call | solution.py:227
  207.9 1.0 copy-done.4
  209.3 134.6 %expert_mirror.1 = (bf16[16,320,384]{2,1,0:T(8,128)(2,1)}, f32[384,1536]{1,0:T(8,128)}, f32[1536,384]{1,0:T(8,128)}, f32[384,128]{1,0:T(8,128)}) custom-call(f32[8,128]{1,0:T(8,128)} %get-tuple-element.28.refs_0_.tot_ref, bf16[32,320,384]{2,1,0:T(8,128)(2,1)} %get-tuple-element.26.refs_1_, bf16[32,320,384]{2,1,0:T(8,128)(2,1)} %get-tuple-element.27.refs_2_, ...), custom_call_target="tpu_custom_call" | custom-call | flops 36238786560 | bytes 33554432 | tf_op jit(solution)/shard_map/expert_mirror/pallas_call | solution.py:227
  343.9 2.4 collective-permute-start.2
  346.9 222.6 %row_return.1 = (bf16[16,320,384]{2,1,0:T(8,128)(2,1)}, bf16[16,320,384]{2,1,0:T(8,128)(2,1)}) custom-call(bf16[16,320,384]{2,1,0:T(8,128)(2,1)} %get-tuple-element.29.go, bf16[16,320,384]{2,1,0:T(8,128)(2,1)} %get-tuple-element.30.gm), custom_call_target="tpu_custom_call" | custom-call | flops 10000000000 | bytes 33554432 | tf_op jit(solution)/shard_map/row_return/pallas_call | solution.py:281
  569.5 67.0 %combine.1 = (bf16[8192,384]{1,0:T(8,128)(2,1)}, f32[384,128]{1,0:T(8,128)}, f32[8,128]{1,0:T(8,128)}) custom-call(s32[64,128]{1,0:T(8,128)} %get-tuple-element.24.slot_ref, f32[8,128]{1,0:T(8,128)} %get-tuple-element.28.refs_0_.tot_ref, bf16[16,320,384]{2,1,0:T(8,128)(2,1)} %get-tuple-element.31.bo, bf16[16,320,384]{2,1,0:T(8,128)(2,1)} %get-tuple-element.32.bm, ...), custom_call_target="tpu_custom_call" | custom-call | tf_op jit(solution)/shard_map/combine/pallas_call | solution.py:434
  636.5 1.2 slice.45
  637.7 1.0 slice_add_fusion
  638.8 0.7 slice_bitcast_fusion
  639.5 0.7 concatenate.18
  640.2 46.6 %psum.7 = f32[12321]{0:T(1024)S(1)} all-reduce(f32[12321]{0:T(1024)S(1)} %concatenate.18), channel_id=1, replica_groups=mesh['ep'=32] {'ep'}, use_global_device_ids=true, to_apply=%region_0.1 | all-reduce | flops 12321 | bytes 98568 | tf_op jit(solution)/shard_map/psum | solution.py:485
  686.8 0.6 slice.55
  687.5 0.7 copy.18
  688.9 1.3 fusion.1
  690.9 3.6 add_bitcast_fusion.1
  694.5 3.4 add_bitcast_fusion
  (23 shorter events, 1.4 us)
Async XLA Ops:
  0.6 207.2 %collective-permute-start = (bf16[384,1536]{1,0:T(8,128)(2,1)}, bf16[384,1536]{1,0:T(8,128)(2,1)S(1)}, u32[]{:S(2)}, u32[]{:S(2)}) collective-permute-start(bf16[384,1536]{1,0:T(8,128)(2,1)} %bitcast.25), channel_id=1, source_target_pairs={{0,16},{1,17},{2,18},{3,19},{4,20},{5,21},{6,22},{7,23},{8,24},{9,... | collective-permute-start | bytes 3538952 | tf_op jit(solution)/shard_map/ppermute | solution.py:468
  4.8 203.1 %collective-permute-start.1 = (bf16[1536,384]{1,0:T(8,128)(2,1)}, bf16[1536,384]{1,0:T(8,128)(2,1)S(1)}, u32[]{:S(2)}, u32[]{:S(2)}) collective-permute-start(bf16[1536,384]{1,0:T(8,128)(2,1)} %bitcast.27), channel_id=1, source_target_pairs={{0,16},{1,17},{2,18},{3,19},{4,20},{5,21},{6,22},{7,23},{8,24},{9,... | collective-permute-start | bytes 3538952 | tf_op jit(solution)/shard_map/ppermute | solution.py:469
  207.9 1.0 copy-start.4
  207.9 1.4 copy-start.5
  343.9 347.0 %collective-permute-start.2 = (f32[384,1536]{1,0:T(8,128)}, f32[384,1536]{1,0:T(8,128)}, u32[]{:S(2)}, u32[]{:S(2)}) collective-permute-start(f32[384,1536]{1,0:T(8,128)} %get-tuple-element.35), channel_id=1, source_target_pairs={{0,16},{1,17},{2,18},{3,19},{4,20},{5,21},{6,22},{7,23},{8,24},{9,... | collective-permute-start | bytes 7077896 | tf_op jit(solution)/shard_map/ppermute | solution.py:479
  346.3 348.2 %collective-permute-start.3 = (f32[1536,384]{1,0:T(8,128)}, f32[1536,384]{1,0:T(8,128)}, u32[]{:S(2)}, u32[]{:S(2)}) collective-permute-start(f32[1536,384]{1,0:T(8,128)} %get-tuple-element.37), channel_id=1, source_target_pairs={{0,16},{1,17},{2,18},{3,19},{4,20},{5,21},{6,22},{7,23},{8,24},{9,... | collective-permute-start | bytes 7077896 | tf_op jit(solution)/shard_map/ppermute | solution.py:480
  569.5 68.3 %copy-start.2 = (f32[384,128]{1,0:T(8,128)S(1)}, f32[384,128]{1,0:T(8,128)}, u32[]{:S(2)}) copy-start(f32[384,128]{1,0:T(8,128)} %get-tuple-element.40) | copy-start | bytes 589828
  569.5 68.3 %copy-start.3 = (f32[384,128]{1,0:T(8,128)S(1)}, f32[384,128]{1,0:T(8,128)}, u32[]{:S(2)}) copy-start(f32[384,128]{1,0:T(8,128)} %get-tuple-element.39) | copy-start | bytes 589828
  569.5 121.4 %copy-start.1 = (f32[384,1536]{1,0:T(8,128)S(1)}, f32[384,1536]{1,0:T(8,128)}, u32[]{:S(2)}) copy-start(f32[384,1536]{1,0:T(8,128)} %get-tuple-element.34) | copy-start | bytes 7077892
  690.9 3.6 copy-start

commit v4 on v3

--- a/solution.py
+++ b/solution.py
@@ -13,6 +13,8 @@
 LANES = 128
 MESH_ID = pl.DeviceIdType.MESH
 VMEM_LIMIT = 60 * 1024 * 1024
+UNROLL = 32
+SLAB = 4
 VM = pl.BlockSpec(memory_space=pltpu.VMEM)
 SM = pl.BlockSpec(memory_space=pltpu.SMEM)
 HBM = pl.BlockSpec(memory_space=pltpu.HBM)
@@ -23,6 +25,12 @@
     for k in (1, 2, 4):
         out = out + k * lax.rem(a // k + b // k, 2)
     return out
+
+
+def hop(i):
+    odd = lax.rem(i, 2)
+    j = (1 - odd) * (7 - i // 2) + odd * ((i + 1) // 2)
+    return j - 7 * (1 - (i + 7) // 8) + 3 * (i // 7)
 
 
 def dot(a, b, ca=1, cb=0):
@@ -47,7 +55,7 @@
     off = 0 if first else hd
 
     def peer_of(j, c):
-        return xor3(chip, j) * 2 + lax.rem(core + c, 2)
+        return xor3(chip, hop(j)) * 2 + lax.rem(core + c, 2)
 
     def token_copy(a, src, dst, peer, slot):
         return pltpu.make_async_remote_copy(
@@ -77,7 +85,7 @@
         token_copy(0, sx, xr, peer, rank).start()
         token_copy(1, sdy, dyr, peer, rank).start()
 
-    start_peer(peer_of(0, 1))
+    start_peer(rank + 1 - 2 * core)
 
     def start_group(j, _):
         start_peer(peer_of(j, 0))
@@ -117,7 +125,7 @@
         def _():
             recv_wait(peer_of(j, 0))
         recv_wait(peer_of(j, 1))
-        pair = xor3(chip, j)
+        pair = xor3(chip, hop(j))
         x = xr[pl.ds(2 * pair, 2)].reshape(rows, d)
         dyf = dyr[pl.ds(2 * pair, 2)].reshape(rows, d).astype(F32)
         lane = lax.broadcasted_iota(jnp.int32, (rows, LANES), 1)
@@ -169,7 +177,7 @@
         token_copy(0, sx, xr, peer, peer).wait_send()
         token_copy(1, sdy, dyr, peer, peer).wait_send()
 
-    send_wait(peer_of(0, 1))
+    send_wait(rank + 1 - 2 * core)
 
     def drain(j, _):
         send_wait(peer_of(j, 0))
@@ -231,15 +239,19 @@
         compiler_params=pltpu.CompilerParams(has_side_effects=True, vmem_limit_bytes=VMEM_LIMIT))(*args)
 
 
-def return_kernel(hd, go, gm, bo, bm, loc_sem, send_sem, recv_sem):
+def return_kernel(cfg, go, gm, x_ref, slot, tot_ref, wr, wrt, gwr_o, gwr_m, bo, bm, gxd_ref, fin,
+                  acc, part, red, loc_sem, send_sem, recv_sem, rs_send, rs_recv, ag_send, ag_recv):
+    hd, n_dev, cap, tb, total_tok = cfg
     me = lax.axis_index('ep')
     half = me // hd
     rank = lax.rem(me, hd)
     chip = rank // 2
     core = lax.rem(rank, 2)
+    t, d = x_ref.shape
+    nk = d // LANES
 
     def peer_of(j, c):
-        return xor3(chip, j) * 2 + lax.rem(core + c, 2)
+        return xor3(chip, hop(j)) * 2 + lax.rem(core + c, 2)
 
     def row_copy(a, peer, slot):
         src, dst = ((go, bo), (gm, bm))[a]
@@ -259,7 +271,7 @@
             row_copy(a, peer, peer).wait_recv()
 
     def each(fn):
-        fn(peer_of(0, 1))
+        fn(rank + 1 - 2 * core)
 
         def body(j, _):
             fn(peer_of(j, 0))
@@ -269,20 +281,91 @@
     each(start)
     for c in own:
         c.start()
+
+    v = tot_ref[0:1, :] * (AUX_WEIGHT * n_dev / (float(total_tok) * total_tok))
+    acc[...] = gwr_o[...] + gwr_m[...]
+    red[...] = jnp.zeros_like(red)
+
+    def block(b, _):
+        at = pl.ds(pl.multiple_of(b * tb, tb), tb)
+        x = x_ref[at, :]
+        lane = lax.broadcasted_iota(jnp.int32, (tb, LANES), 1)
+        p, lz = router_rows(x, wr, lane, n_dev)
+        dl = base_grad(p, lz, v, 2.0 * Z_WEIGHT / total_tok)
+        dl2, dl3 = split_rows(dl)
+        gxd_ref[at, :] = dot(dl3, wrt[...]).astype(BF)
+        drop = (slot[pl.ds(b, 1), :] >= n_dev * cap).astype(F32)
+        drop = jnp.broadcast_to(drop, (LANES, LANES)).T.astype(BF)
+        gw = dot(x.T, dl2 * jnp.concatenate([drop, drop], axis=1))
+        acc[...] += gw[:, :LANES] + gw[:, LANES:]
+        red[0:1, :] += jnp.sum(p, axis=0, keepdims=True)
+        red[1:2, :] += jnp.sum(jnp.broadcast_to(lz * lz, (tb, LANES)), axis=0, keepdims=True)
+        return 0
+    lax.fori_loop(0, t // tb, block, 0)
+
+    gt = acc[...].T
+    part[...] = jnp.zeros_like(part)
+    for k in range(nk):
+        part[pl.ds(k, n_dev, stride=8), :] = gt[0:n_dev, k * LANES:(k + 1) * LANES]
+    for k in (0, 1):
+        part[pl.ds(nk + k, n_dev, stride=8), :] = jnp.broadcast_to(red[k:k + 1, :], (n_dev, LANES))
+
+    def tile(ref, i):
+        return ref.at[pl.ds(pl.multiple_of(i * 8, 8), 8)]
+
+    def rs_copy(k, slot):
+        peer = lax.rem(me + k, n_dev)
+        at = me if slot else peer
+        return pltpu.make_async_remote_copy(
+            src_ref=tile(part, peer), dst_ref=tile(fin, n_dev + at), send_sem=rs_send.at[peer],
+            recv_sem=rs_recv.at[at], device_id=(peer,), device_id_type=MESH_ID)
+
+    def ag_copy(k, slot):
+        peer = lax.rem(me + k, n_dev)
+        at = me if slot else peer
+        return pltpu.make_async_remote_copy(
+            src_ref=red, dst_ref=tile(fin, at), send_sem=ag_send.at[peer],
+            recv_sem=ag_recv.at[at], device_id=(peer,), device_id_type=MESH_ID)
+
+    def others(fn):
+        def body(k, _):
+            fn(k)
+            return 0
+        lax.fori_loop(1, n_dev, body, 0)
+    others(lambda k: rs_copy(k, True).start())
+    mine = pl.ds(pl.multiple_of(me * 8, 8), 8)
+    red[...] = part[mine, :]
+
+    def collect(k):
+        rs_copy(k, False).wait_recv()
+        src = lax.rem(me + k, n_dev)
+        red[...] += fin[pl.ds(pl.multiple_of((n_dev + src) * 8, 8), 8), :]
+    others(collect)
+    others(lambda k: ag_copy(k, True).start())
+    fin[mine, :] = red[...]
+    others(lambda k: ag_copy(k, False).wait_recv())
+    others(lambda k: rs_copy(k, False).wait_send())
+    others(lambda k: ag_copy(k, False).wait_send())
     for c in own:
         c.wait()
     each(wait)
 
 
-def return_call(go, gm):
-    hd = go.shape[0]
+def return_call(go, gm, x, slot, tot, wr, wrt, gwr_o, gwr_m, total_tok):
+    hd, cap, d = go.shape
+    n_dev = 2 * hd
     dma = pltpu.SemaphoreType.DMA
-    sd = jax.ShapeDtypeStruct(go.shape, BF)
+    sd = jax.ShapeDtypeStruct
+    row = sd(go.shape, BF)
     return pl.pallas_call(
-        functools.partial(return_kernel, hd), out_shape=[sd, sd], in_specs=[HBM, HBM], out_specs=[HBM, HBM],
-        scratch_shapes=[dma((2,)), dma((2, hd)), dma((2, hd))], name='row_return',
+        functools.partial(return_kernel, (hd, n_dev, cap, LANES, total_tok)),
+        out_shape=[row, row, sd(x.shape, BF), sd((2 * n_dev * 8, LANES), F32)],
+        in_specs=[HBM, HBM] + [VM] * 7, out_specs=[HBM, HBM, VM, VM],
+        scratch_shapes=[pltpu.VMEM((d, LANES), F32), pltpu.VMEM((n_dev * 8, LANES), F32), pltpu.VMEM((8, LANES), F32),
+                        dma((2,)), dma((2, hd)), dma((2, hd))] + [dma((n_dev,))] * 4, name='row_return',
         cost_estimate=pl.CostEstimate(flops=10 ** 10, bytes_accessed=32 * 2 ** 20, transcendentals=0),
-        compiler_params=pltpu.CompilerParams(has_side_effects=True))(go, gm)
+        compiler_params=pltpu.CompilerParams(has_side_effects=True, vmem_limit_bytes=VMEM_LIMIT))(
+            go, gm, x, slot, tot, wr, wrt, gwr_o, gwr_m)
 
 
 def route_kernel(ne, cap, half_ref, idx_ref, slot_ref, cnt_ref, hot, cum):
@@ -331,13 +414,14 @@
             tmp[pl.ds(4 + k, tb, stride=8), :] = df[:, k * LANES:(k + 1) * LANES]
 
         def place(q, _):
-            row = i * (tb // LANES) + q // (LANES // 16)
-            col = lax.rem(q, LANES // 16) * 16
-            for u in range(16):
-                s = slot_ref[row, col + u]
-                big[pl.ds(pl.multiple_of(s * 8, 8), 8), :] = tmp[pl.ds(pl.multiple_of((q * 16 + u) * 8, 8), 8), :]
-            return 0
-        lax.fori_loop(0, tb // 16, place, 0)
+            row = i * (tb // LANES) + q // (LANES // UNROLL)
+            col = lax.rem(q, LANES // UNROLL) * UNROLL
+            at = [slot_ref[row, col + u] * 8 for u in range(UNROLL)]
+            rows = tmp[pl.ds(pl.multiple_of(q * (8 * UNROLL), 8), 8 * UNROLL), :]
+            for u in range(UNROLL):
+                big[pl.ds(pl.multiple_of(at[u], 8), 8), :] = rows[8 * u:8 * u + 8]
+            return 0
+        lax.fori_loop(0, tb // UNROLL, place, 0)
 
     @pl.when(i >= nb)
     def _():
@@ -366,23 +450,21 @@
         compiler_params=pltpu.CompilerParams(vmem_limit_bytes=VMEM_LIMIT))(slot, cnt, x, dy)
 
 
-def combine_kernel(cfg, slot_ref, tot_ref, bo, bm, x_ref, wr, wrt, gx_ref, gwr, stat, tmp, big):
-    nb, tb, n_dev, hd, cap, d, total_tok = cfg
+def combine_kernel(cfg, slot_ref, bo, bm, gxd, gx_ref, tmp, big):
+    tb, n_dev, hd, cap, d = cfg
     i = pl.program_id(0)
     nk = d // LANES
 
     def put(rows, e):
         f = rows.astype(F32)
-        base = e * (cap * 8)
+        base = e * (cap * SLAB)
         for k in range(nk):
-            big[pl.ds(base + k, cap, stride=8), :] = f[:, k * LANES:(k + 1) * LANES]
-        big[pl.ds(base + nk, cap, stride=8), :] = jnp.zeros((cap, LANES), F32)
+            big[pl.ds(base + k, cap, stride=SLAB), :] = f[:, k * LANES:(k + 1) * LANES]
+        big[pl.ds(base + nk, cap, stride=SLAB), :] = jnp.zeros((cap, LANES), F32)
 
     @pl.when(i == 0)
     def _():
-        big[n_dev * cap * 8:n_dev * cap * 8 + 8, :] = jnp.ones((8, LANES), F32)
-        gwr[...] = jnp.zeros_like(gwr)
-        stat[...] = jnp.zeros_like(stat)
+        big[n_dev * cap * SLAB:n_dev * cap * SLAB + 8, :] = jnp.ones((8, LANES), F32)
 
     @pl.when(i < hd)
     def _():
@@ -397,48 +479,34 @@
         b = i - n_dev
 
         def fetch(q, _):
-            row = b * (tb // LANES) + q // (LANES // 16)
-            col = lax.rem(q, LANES // 16) * 16
-            for u in range(16):
-                s = slot_ref[row, col + u]
-                tmp[pl.ds(pl.multiple_of((q * 16 + u) * 8, 8), 8), :] = big[pl.ds(pl.multiple_of(s * 8, 8), 8), :]
-            return 0
-        lax.fori_loop(0, tb // 16, fetch, 0)
-        x = x_ref[...]
-        lane = lax.broadcasted_iota(jnp.int32, (tb, LANES), 1)
-        p, lz = router_rows(x, wr, lane, n_dev)
-        v = tot_ref[0:1, :] * (AUX_WEIGHT * n_dev / (float(total_tok) * total_tok))
-        dl = base_grad(p, lz, v, 2.0 * Z_WEIGHT / total_tok)
-        _, dl3 = split_rows(dl)
-        gxd = dot(dl3, wrt[...])
-        drop = tmp[pl.ds(nk, tb, stride=8), :]
-        dl2, _ = split_rows(dl * drop)
-        gw = lax.dot_general(x, dl2, (((0,), (0,)), ((), ())), preferred_element_type=F32)
-        gwr[...] += gw[:, :LANES] + gw[:, LANES:]
-        stat[0:1, :] += jnp.sum(p, axis=0, keepdims=True)
-        stat[1:2, :] += jnp.sum(jnp.broadcast_to(lz * lz, (tb, LANES)), axis=0, keepdims=True)
+            row = b * (tb // LANES) + q // (LANES // UNROLL)
+            col = lax.rem(q, LANES // UNROLL) * UNROLL
+            at = [slot_ref[row, col + u] * SLAB for u in range(UNROLL)]
+            rows = [big[pl.ds(pl.multiple_of(at[u], SLAB), SLAB), :] for u in range(UNROLL)]
+            tmp[pl.ds(pl.multiple_of(q * (SLAB * UNROLL), 8), SLAB * UNROLL), :] = jnp.concatenate(rows, axis=0)
+            return 0
+        lax.fori_loop(0, tb // UNROLL, fetch, 0)
+        drop = tmp[pl.ds(nk, tb, stride=SLAB), :] > 0.5
         for k in range(nk):
-            got = tmp[pl.ds(k, tb, stride=8), :]
-            gx_ref[:, k * LANES:(k + 1) * LANES] = jnp.where(drop > 0.5, gxd[:, k * LANES:(k + 1) * LANES], got).astype(BF)
-
-
-def combine_call(slot, tot, bo, bm, x, wr, wrt, total_tok):
-    t, d = x.shape
+            lanes = slice(k * LANES, (k + 1) * LANES)
+            got = tmp[pl.ds(k, tb, stride=SLAB), :]
+            gx_ref[:, lanes] = jnp.where(drop, gxd[:, lanes].astype(F32), got).astype(BF)
+
+
+def combine_call(slot, bo, bm, gxd):
+    t, d = gxd.shape
     hd, cap, _ = bo.shape
     n_dev = 2 * hd
     tb = 512
-    nb = t // tb
-    sd = jax.ShapeDtypeStruct
     tok = pl.BlockSpec((tb, d), lambda i: (jnp.maximum(i - n_dev, 0), 0))
-    const = lambda s: pl.BlockSpec(s, lambda i: (0, 0))
     return pl.pallas_call(
-        functools.partial(combine_kernel, (nb, tb, n_dev, hd, cap, d, total_tok)), grid=(n_dev + nb,),
-        out_shape=[sd((t, d), BF), sd((d, LANES), F32), sd((8, LANES), F32)],
-        in_specs=[SM, VM, pl.BlockSpec((1, cap, d), lambda i: (jnp.minimum(i, hd - 1), 0, 0)),
-                  pl.BlockSpec((1, cap, d), lambda i: (jnp.clip(i - hd, 0, hd - 1), 0, 0)), tok, VM, VM],
-        out_specs=[tok, const((d, LANES)), const((8, LANES))],
-        scratch_shapes=[pltpu.VMEM((tb * 8, LANES), F32), pltpu.VMEM((n_dev * cap * 8 + 8, LANES), F32)], name='combine',
-        compiler_params=pltpu.CompilerParams(vmem_limit_bytes=VMEM_LIMIT))(slot, tot, bo, bm, x, wr, wrt)
+        functools.partial(combine_kernel, (tb, n_dev, hd, cap, d)), grid=(n_dev + t // tb,),
+        out_shape=jax.ShapeDtypeStruct((t, d), BF),
+        in_specs=[SM, pl.BlockSpec((1, cap, d), lambda i: (jnp.minimum(i, hd - 1), 0, 0)),
+                  pl.BlockSpec((1, cap, d), lambda i: (jnp.clip(i - hd, 0, hd - 1), 0, 0)), tok],
+        out_specs=tok,
+        scratch_shapes=[pltpu.VMEM((tb * SLAB, LANES), F32), pltpu.VMEM((n_dev * cap * SLAB + 8, LANES), F32)], name='combine',
+        compiler_params=pltpu.CompilerParams(vmem_limit_bytes=VMEM_LIMIT))(slot, bo, bm, gxd)
 
 
 def split_router(w_router):
@@ -478,15 +546,13 @@
         gx_m, gwi_m, gwo_m, gwr_m = expert_call(base + (False,), tot, sx, sdy, w_in_m, w_out_m, wr, wrt)
         gwi_r = lax.ppermute(gwi_m, 'ep', mirror)
         gwo_r = lax.ppermute(gwo_m, 'ep', mirror)
-        back_o, back_m = return_call(gx_o, gx_m)
-        grad_x, gwr_d, stat = combine_call(slot, tot, back_o, back_m, x_tokens, wr, wrt, total_tok)
-
-        fin = jnp.concatenate([(gwr_d + gwr_m + gwr_o)[:, :ne].reshape(-1), stat[0, :ne], stat[1, :1]])
-        fin = lax.psum(fin, 'ep')
-        nr = d_model * ne
-        grad_w_router = fin[:nr].reshape(d_model, ne)
-        aux_loss = AUX_WEIGHT * ne * jnp.sum(tot[0, :ne] / total_tok * fin[nr:nr + ne] / total_tok)
-        z_loss = Z_WEIGHT * fin[nr + ne] / total_tok
+        back_o, back_m, gx_drop, fin = return_call(gx_o, gx_m, x_tokens, slot, tot, wr, wrt, gwr_o, gwr_m, total_tok)
+        grad_x = combine_call(slot, back_o, back_m, gx_drop)
+        fin = fin[:ne * 8].reshape(ne, 8, LANES)
+        nk = d_model // LANES
+        grad_w_router = fin[:, :nk].reshape(ne, d_model).T
+        aux_loss = AUX_WEIGHT * ne * jnp.sum(tot[0, :ne] / total_tok * fin[0, nk, :ne] / total_tok)
+        z_loss = Z_WEIGHT * fin[0, nk + 1, 0] / total_tok
         return grad_x, (gwi_o + gwi_r)[None], (gwo_o + gwo_r)[None], grad_w_router, aux_loss, z_loss
 
     return jax.shard_map(expert_layer, mesh=mesh,

time: 702 us -> 605 us (0.86)
  Pallas kernels: 623 us -> 576 us
  blocking collectives: 46.6 us -> 0 us
    psum x1 -> x0, blocking collectives: 46.6 us -> none  [expert_layer(): fin = lax.psum(fin, 'ep')]
    pallas_call x2, Pallas kernels: 281 us -> 259 us  [expert_call(): pl.pallas_call(functools.partial(expert_kernel, cfg), out_shape=out_shape...]
    pallas_call x2, Pallas kernels: 290 us -> 268 us  [the longest x1 223 us: return_call(): pl.pallas_call(functools.partial(return_kernel, (hd, n_dev, cap, LANES, t...]
  transfers between devices with their start and end apart: 4 -> 4, of which waited for: 0 -> 0; matrix products, arithmetic and copies ran while one was open for 2% -> 2% of each run, Pallas kernels for 70% -> 78%
where the time goes in v4:
time: 605 us; the launch traced here: 604 us
  Pallas kernels  576 us (95%)
  other arithmetic  11.8 us (2%)
  starting transfers between devices  7.23 us (1%)
    pallas_call x2, Pallas kernels, expert_call(): pl.pallas_call(functools.partial(expert_kernel, cfg), out_shape=out_shape...  259 us
    pallas_call x1, Pallas kernels, return_call(): pl.pallas_call(functools.partial(return_kernel, (hd, n_dev, cap, LANES, t...  223 us
    pallas_call x1, Pallas kernels, dispatch_call(): pl.pallas_call(functools.partial(dispatch_kernel, nb, tb, ne, cap, d), gr...  47.8 us
    pallas_call x1, Pallas kernels, combine_call(): pl.pallas_call(functools.partial(combine_kernel, (tb, n_dev, hd, cap, d))...  44.8 us
  transfers between devices with their start and end apart: 4, of which 0 were waited for; matrix products, arithmetic and copies ran while one was open for 2% of the time, Pallas kernels for 78%

profile of v4, /device:TPU:0, one launch (start us, length us, event | category | flops | bytes accessed | tf_op | source)
XLA Modules:
  0.0 604.0 jit_solution(12953844046751361718)
XLA Ops:
  0.6 4.2 collective-permute-start
  4.8 0.1 collective-permute-start.1
  4.9 0.8 fusion.3
  5.7 0.7 maximum_bitcast_fusion.refs_6_.wrt
  6.5 2.0 route.1
  8.5 0.7 slice_convert_fusion
  9.2 0.1 slice_bitcast_fusion.3
  9.2 0.8 copy.15.refs_5_.wr
  10.0 1.3 broadcast_select_fusion.cnt_ref
  11.3 47.8 %dispatch.1 = (bf16[32,320,384]{2,1,0:T(8,128)(2,1)}, bf16[32,320,384]{2,1,0:T(8,128)(2,1)}) custom-call(s32[64,128]{1,0:T(8,128)} %get-tuple-element.23.slot_ref.slot, s32[32]{0:T(128)} %broadcast_select_fusion.cnt_ref, bf16[8192,384]{1,0:T(8,128)(2,1)} %x_ref.3, bf16[8192,384]{1,0:T(8,128)(2,1)} %dy_ref.1), custom_call_target="tpu_custom_call" | custom-call | tf_op jit(solution)/shard_map/dispatch/pallas_call | solution.py:446
  59.1 152.9 %expert_own.1 = (bf16[16,320,384]{2,1,0:T(8,128)(2,1)}, f32[384,1536]{1,0:T(8,128)}, f32[1536,384]{1,0:T(8,128)}, f32[384,128]{1,0:T(8,128)}, f32[8,128]{1,0:T(8,128)}) custom-call(f32[8,128]{1,0:T(8,128)} %get-tuple-element.24.refs_0_, bf16[32,320,384]{2,1,0:T(8,128)(2,1)} %get-tuple-element.25.refs_1_, bf16[32,320,384]{2,1,0:T(8,128)(2,1)} %get-tuple-element.26.refs_2_, ...), custom_call_target="tpu_custom_call" | custom-call | flops 36238786560 | bytes 33554432 | tf_op jit(solution)/shard_map/expert_own/pallas_call | solution.py:235
  212.1 1.0 copy-done.2
  213.1 0.4 copy-done.3
  213.5 105.7 %expert_mirror.1 = (bf16[16,320,384]{2,1,0:T(8,128)(2,1)}, f32[384,1536]{1,0:T(8,128)}, f32[1536,384]{1,0:T(8,128)}, f32[384,128]{1,0:T(8,128)}) custom-call(f32[8,128]{1,0:T(8,128)} %get-tuple-element.28.refs_0_.tot_ref, bf16[32,320,384]{2,1,0:T(8,128)(2,1)} %get-tuple-element.25.refs_1_, bf16[32,320,384]{2,1,0:T(8,128)(2,1)} %get-tuple-element.26.refs_2_, ...), custom_call_target="tpu_custom_call" | custom-call | flops 36238786560 | bytes 33554432 | tf_op jit(solution)/shard_map/expert_mirror/pallas_call | solution.py:235
  319.2 2.5 collective-permute-start.2
  321.8 0.4 collective-permute-start.3
  322.2 223.0 %row_return.1 = (bf16[16,320,384]{2,1,0:T(8,128)(2,1)}, bf16[16,320,384]{2,1,0:T(8,128)(2,1)}, bf16[8192,384]{1,0:T(8,128)(2,1)}, f32[512,128]{1,0:T(8,128)}) custom-call(bf16[16,320,384]{2,1,0:T(8,128)(2,1)} %get-tuple-element.27.go, bf16[16,320,384]{2,1,0:T(8,128)(2,1)} %get-tuple-element.29.gm, bf16[8192,384]{1,0:T(8,128)(2,1)} %x_ref.3, ...), custom_call_target="tpu_custom_call" | custom-call | flops 10000000000 | bytes 33554432 | tf_op jit(solution)/shard_map/row_return/pallas_call | solution.py:360
  545.2 0.9 slice_bitcast_fusion
  546.1 0.5 slice.44
  546.7 0.6 copy.20
  547.9 1.3 fusion.2
  549.9 44.8 %combine.1 = bf16[8192,384]{1,0:T(8,128)(2,1)} custom-call(s32[64,128]{1,0:T(8,128)} %get-tuple-element.23.slot_ref.slot, bf16[16,320,384]{2,1,0:T(8,128)(2,1)} %get-tuple-element.32.bo, bf16[16,320,384]{2,1,0:T(8,128)(2,1)} %get-tuple-element.33.bm, bf16[8192,384]{1,0:T(8,128)(2,1)} %get-tuple-element.34.gxd), custom_call_target="tpu_custom_call" | custom-call | tf_op jit(solution)/shard_map/combine/pallas_call | solution.py:502
  594.7 3.6 add_bitcast_fusion.1
  598.3 3.4 add_bitcast_fusion
  (13 shorter events, 0.1 us)
Async XLA Ops:
  0.6 211.5 %collective-permute-start = (bf16[384,1536]{1,0:T(8,128)(2,1)}, bf16[384,1536]{1,0:T(8,128)(2,1)S(1)}, u32[]{:S(2)}, u32[]{:S(2)}) collective-permute-start(bf16[384,1536]{1,0:T(8,128)(2,1)} %bitcast.41), channel_id=1, source_target_pairs={{0,16},{1,17},{2,18},{3,19},{4,20},{5,21},{6,22},{7,23},{8,24},{9,... | collective-permute-start | bytes 3538952 | tf_op jit(solution)/shard_map/ppermute | solution.py:536
  4.8 207.3 %collective-permute-start.1 = (bf16[1536,384]{1,0:T(8,128)(2,1)}, bf16[1536,384]{1,0:T(8,128)(2,1)S(1)}, u32[]{:S(2)}, u32[]{:S(2)}) collective-permute-start(bf16[1536,384]{1,0:T(8,128)(2,1)} %bitcast.43), channel_id=1, source_target_pairs={{0,16},{1,17},{2,18},{3,19},{4,20},{5,21},{6,22},{7,23},{8,24},{9,... | collective-permute-start | bytes 3538952 | tf_op jit(solution)/shard_map/ppermute | solution.py:537
  212.1 1.0 copy-start.2
  212.1 1.4 copy-start.3
  319.2 275.4 %collective-permute-start.2 = (f32[384,1536]{1,0:T(8,128)}, f32[384,1536]{1,0:T(8,128)}, u32[]{:S(2)}, u32[]{:S(2)}) collective-permute-start(f32[384,1536]{1,0:T(8,128)} %get-tuple-element.36), channel_id=1, source_target_pairs={{0,16},{1,17},{2,18},{3,19},{4,20},{5,21},{6,22},{7,23},{8,24},{9,... | collective-permute-start | bytes 7077896 | tf_op jit(solution)/shard_map/ppermute | solution.py:547
  321.8 276.5 %collective-permute-start.3 = (f32[1536,384]{1,0:T(8,128)}, f32[1536,384]{1,0:T(8,128)}, u32[]{:S(2)}, u32[]{:S(2)}) collective-permute-start(f32[1536,384]{1,0:T(8,128)} %get-tuple-element.38), channel_id=1, source_target_pairs={{0,16},{1,17},{2,18},{3,19},{4,20},{5,21},{6,22},{7,23},{8,24},{9,... | collective-permute-start | bytes 7077896 | tf_op jit(solution)/shard_map/ppermute | solution.py:548
  549.9 44.8 %copy-start.1 = (f32[384,1536]{1,0:T(8,128)S(1)}, f32[384,1536]{1,0:T(8,128)}, u32[]{:S(2)}) copy-start(f32[384,1536]{1,0:T(8,128)} %get-tuple-element.35) | copy-start | bytes 7077892
  594.7 3.6 copy-start

commit v5 on v4

v5 whole, which is shorter than its diff:
```python
import functools
import jax
import jax.numpy as jnp
from jax import lax
from jax.experimental import pallas as pl
from jax.experimental.pallas import tpu as pltpu
from jax.sharding import PartitionSpec as P

AUX_WEIGHT = 0.01
Z_WEIGHT = 0.001
BF = jnp.bfloat16
F32 = jnp.float32
LANES = 128
MESH_ID = pl.DeviceIdType.MESH
VMEM_LIMIT = 60 * 1024 * 1024
UNROLL = 32
SLAB = 4
VM = pl.BlockSpec(memory_space=pltpu.VMEM)
SM = pl.BlockSpec(memory_space=pltpu.SMEM)
HBM = pl.BlockSpec(memory_space=pltpu.HBM)


def xor3(a, b):
    out = 0
    for k in (1, 2, 4):
        out = out + k * lax.rem(a // k + b // k, 2)
    return out


def hop(i):
    odd = lax.rem(i, 2)
    j = (1 - odd) * (7 - i // 2) + odd * ((i + 1) // 2)
    return j - 7 * (1 - (i + 7) // 8) + 3 * (i // 7)


def dot(a, b, ca=1, cb=0):
    return lax.dot_general(a, b, (((ca,), (cb,)), ((), ())), preferred_element_type=F32)


def expert_kernel(cfg, *refs):
    n_dev, hd, cap, d, ff, ft, total_tok = cfg
    (cnt_ref, sx, sdy, wi_o, wo_o, wi_m, wr, wrt,
     gx_out, gwi_o, gwo_o, gwi_m, gwo_m, gwr, tot_ref,
     cbuf, wo_m, xr, dyr, gwot, dlw, oacc, dracc, gb, xt, gt,
     csend, crecv, loc_sem, send_sem, recv_sem, out_sem, w_send, w_recv) = refs
    me = lax.axis_index('ep')
    half = me // hd
    rank = lax.rem(me, hd)
    chip = rank // 2
    core = lax.rem(rank, 2)
    n_grp = hd // 2
    rows = 2 * cap
    twin = rank + 1 - 2 * core
    mirror = lax.rem(me + hd, n_dev)

    def peer_of(j, c):
        return xor3(chip, hop(j)) * 2 + lax.rem(core + c, 2)

    def token_copy(part, a, peer, slot):
        src, dst = ((sx, xr), (sdy, dyr))[a]
        off = part * hd
        return pltpu.make_async_remote_copy(
            src_ref=src.at[off + peer], dst_ref=dst.at[off + slot], send_sem=send_sem.at[a, off + peer],
            recv_sem=recv_sem.at[a, off + slot], device_id=(half * hd + peer,), device_id_type=MESH_ID)

    def count_copy(k, sending):
        peer = lax.rem(me + k, n_dev)
        slot = me if sending else peer
        return pltpu.make_async_remote_copy(
            src_ref=cnt_ref, dst_ref=cbuf.at[slot], send_sem=csend.at[peer],
            recv_sem=crecv.at[slot], device_id=(peer,), device_id_type=MESH_ID)

    def others(fn):
        def body(k, _):
            fn(k)
            return 0
        lax.fori_loop(1, n_dev, body, 0)

    def each(fn):
        fn(twin)

        def body(j, _):
            fn(peer_of(j, 0))
            fn(peer_of(j, 1))
            return 0
        lax.fori_loop(1, n_grp, body, 0)

    weight = pltpu.make_async_remote_copy(src_ref=wo_o, dst_ref=wo_m, send_sem=w_send, recv_sem=w_recv,
                                          device_id=(mirror,), device_id_type=MESH_ID)
    others(lambda k: count_copy(k, True).start())
    cbuf[me] = cnt_ref[...]
    own = [pltpu.make_async_copy(src.at[q * hd + rank], dst.at[q * hd + rank], loc_sem.at[q, a])
           for q in (0, 1) for a, (src, dst) in enumerate(((sx, xr), (sdy, dyr)))]
    for c in own:
        c.start()

    def start(part):
        def one(peer):
            token_copy(part, 0, peer, rank).start()
            token_copy(part, 1, peer, rank).start()
        each(one)
    start(0)
    weight.start()
    start(1)

    gwr[...] = jnp.zeros_like(gwr)
    others(lambda k: count_copy(k, False).wait_recv())
    tot_ref[...] = jnp.sum(cbuf[...], axis=0)
    v = tot_ref[0:1, :] * (AUX_WEIGHT * n_dev / (float(total_tok) * total_tok))
    zc = 2.0 * Z_WEIGHT / total_tok

    for part, (e_id, wi, wo, gwi, gwo) in enumerate(((me, wi_o, wo_o, gwi_o, gwo_o), (mirror, wi_m, wo_m, gwi_m, gwo_m))):
        gwi[...] = jnp.zeros_like(gwi)
        gwot[...] = jnp.zeros_like(gwot)
        if part:
            weight.wait_recv()

        def recv_wait(peer):
            token_copy(part, 0, peer, peer).wait_recv()
            token_copy(part, 1, peer, peer).wait_recv()

        def group(j, _):
            @pl.when(j == 0)
            def _():
                own[2 * part].wait()
                own[2 * part + 1].wait()

            @pl.when(j > 0)
            def _():
                recv_wait(peer_of(j, 0))
            recv_wait(peer_of(j, 1))
            pair = part * n_grp + xor3(chip, hop(j))
            two = pl.ds(2 * pair, 2)
            x = xr[two].reshape(rows, d)
            dyf = dyr[two].reshape(rows, d).astype(F32)
            lane = lax.broadcasted_iota(jnp.int32, (rows, LANES), 1)
            p, lz = router_rows(x, wr, lane, n_dev)
            hot = (lane == e_id).astype(F32)
            gate = jnp.sum(p * hot, axis=1, keepdims=True)
            g = (gate * dyf).astype(BF)
            gb[...] = g
            xt[...] = x.T
            gt[...] = g.T
            oacc[...] = jnp.zeros_like(oacc)
            dracc[...] = jnp.zeros_like(dracc)

            def ff_tile(f, _):
                fo = pl.multiple_of(f * ft, ft)
                wit = wi[:, pl.ds(fo, ft)]
                wot = wo[pl.ds(fo, ft), :]
                xx = xr[two].reshape(rows, d)
                h = jnp.maximum(dot(xx, wit), 0.0).astype(BF)
                oacc[...] += dot(h, wot)
                dh = dot(gb[...], wot, 1, 1)
                da = jnp.where(h > 0, dh, 0.0).astype(BF)
                dracc[...] += dot(da, wit, 1, 1)
                gwot[:, pl.ds(fo, ft)] += dot(gt[...], h)
                gwi[:, pl.ds(fo, ft)] += dot(xt[...], da)
                return 0
            lax.fori_loop(0, ff // ft, ff_tile, 0)

            o = oacc[...].astype(BF).astype(F32)
            dgate = jnp.sum(o * dyr[two].reshape(rows, d).astype(F32), axis=1, keepdims=True)
            dl = (gate * dgate) * (hot - p) + base_grad(p, lz, v, zc)
            dl2, dl3 = split_rows(dl)
            dlw[...] = dot(dl3, wrt[...])
            gw = dot(xt[...], dl2)
            gwr[...] += gw[:, :LANES] + gw[:, LANES:]
            gx = (dracc[...].astype(BF).astype(F32) + dlw[...]).astype(BF)
            dyr[two] = gx.reshape(2, cap, d)
            pltpu.make_async_copy(dyr.at[two], gx_out.at[two], out_sem.at[pair]).start()
            return 0
        lax.fori_loop(0, n_grp, group, 0)

        def finish(f, _):
            fo = pl.multiple_of(f * ft, ft)
            gwo[pl.ds(fo, ft), :] = gwot[:, pl.ds(fo, ft)].T
            return 0
        lax.fori_loop(0, ff // ft, finish, 0)

    for part in (0, 1):
        def drain(peer):
            token_copy(part, 0, peer, peer).wait_send()
            token_copy(part, 1, peer, peer).wait_send()
        each(drain)
    weight.wait_send()

    def out_wait(s, _):
        pltpu.make_async_copy(dyr.at[pl.ds(2 * s, 2)], gx_out.at[pl.ds(2 * s, 2)], out_sem.at[s]).wait()
        return 0
    lax.fori_loop(0, 2 * n_grp, out_wait, 0)
    others(lambda k: count_copy(k, False).wait_send())


def router_rows(x, wr, lane, n_dev):
    lg = dot(x, wr[...])
    lg = jnp.where(lane < n_dev, lg[:, :LANES] + lg[:, LANES:], -1e30)
    mx = jnp.max(lg, axis=1, keepdims=True)
    ex = jnp.exp(lg - mx)
    sm = jnp.sum(ex, axis=1, keepdims=True)
    return ex / sm, mx + jnp.log(sm)


def base_grad(p, lz, v, zc):
    spread = jnp.sum(p * v, axis=1, keepdims=True)
    return p * (v - spread) + (zc * lz) * p


def split_rows(dl):
    hi = dl.astype(BF)
    lo = (dl - hi.astype(F32)).astype(BF)
    dl2 = jnp.concatenate([hi, lo], axis=1)
    return dl2, jnp.concatenate([dl2, hi], axis=1)


def expert_call(cfg, *args):
    n_dev, hd, cap, d, ff, ft, total_tok = cfg
    sd = jax.ShapeDtypeStruct
    rows = 2 * cap
    dma = pltpu.SemaphoreType.DMA
    vf = lambda *shape: pltpu.VMEM(shape, F32)
    vb = lambda *shape: pltpu.VMEM(shape, BF)
    scratch = [vf(n_dev, 8, LANES), vb(ff, d), vb(n_dev, cap, d), vb(n_dev, cap, d), vf(d, ff), vf(rows, d), vf(rows, d), vf(rows, d),
               vb(rows, d), vb(d, rows), vb(d, rows), dma((n_dev,)), dma((n_dev,)), dma((2, 2)), dma((2, n_dev)), dma((2, n_dev)),
               dma((hd,)), dma, dma]
    wi, wo = sd((d, ff), F32), sd((ff, d), F32)
    return pl.pallas_call(
        functools.partial(expert_kernel, cfg),
        out_shape=[sd((n_dev, cap, d), BF), wi, wo, wi, wo, sd((d, LANES), F32), sd((8, LANES), F32)],
        in_specs=[VM, HBM, HBM] + [VM] * 5, out_specs=[HBM] + [VM] * 6, scratch_shapes=scratch, name='experts',
        cost_estimate=pl.CostEstimate(flops=24 * hd * cap * d * ff, bytes_accessed=64 * 2 ** 20, transcendentals=0),
        compiler_params=pltpu.CompilerParams(has_side_effects=True, vmem_limit_bytes=VMEM_LIMIT))(*args)


def finish_kernel(cfg, slot_sm, rows, gwi, gwo, x_ref, slot, tot_ref, wr, wrt, gwr, gx_ref, gwi_r, gwo_r, fin,
                  bo, bm, big, tmp, acc, part, red, loc_sem, send_sem, recv_sem, rs_send, rs_recv, ag_send, ag_recv,
                  gr_send, gr_recv):
    hd, n_dev, cap, tb, total_tok = cfg
    me = lax.axis_index('ep')
    half = me // hd
    rank = lax.rem(me, hd)
    chip = rank // 2
    core = lax.rem(rank, 2)
    t, d = x_ref.shape
    nk = d // LANES

    def peer_of(j, c):
        return xor3(chip, hop(j)) * 2 + lax.rem(core + c, 2)

    def row_copy(a, peer, slot):
        dst = (bo, bm)[a]
        return pltpu.make_async_remote_copy(
            src_ref=rows.at[a * hd + peer], dst_ref=dst.at[slot], send_sem=send_sem.at[a, peer],
            recv_sem=recv_sem.at[a, slot], device_id=(half * hd + peer,), device_id_type=MESH_ID)

    own = [pltpu.make_async_copy(rows.at[a * hd + rank], b.at[rank], loc_sem.at[a]) for a, b in enumerate((bo, bm))]

    def grad_copy(a):
        src, dst = ((gwo, gwo_r), (gwi, gwi_r))[a]
        return pltpu.make_async_remote_copy(
            src_ref=src, dst_ref=dst, send_sem=gr_send.at[a], recv_sem=gr_recv.at[a],
            device_id=(lax.rem(me + hd, n_dev),), device_id_type=MESH_ID)

    def put(buf, base, s):
        f = buf[s].astype(F32)
        at = pl.ds((base + s) * cap, cap)
        for k in range(nk):
            big[at, k, :] = f[:, k * LANES:(k + 1) * LANES]
        big[at, nk, :] = jnp.zeros((cap, LANES), F32)

    def start(peer):
        for a in (0, 1):
            row_copy(a, peer, rank).start()

    def wait(peer):
        for a in (0, 1):
            row_copy(a, peer, peer).wait_recv()
            put((bo, bm)[a], a * hd, peer)

    def drain(peer):
        for a in (0, 1):
            row_copy(a, peer, peer).wait_send()

    def each(fn):
        fn(rank + 1 - 2 * core)

        def body(j, _):
            fn(peer_of(j, 0))
            fn(peer_of(j, 1))
            return 0
        lax.fori_loop(1, hd // 2, body, 0)
    each(start)
    grad_copy(0).start()
    for c in own:
        c.start()

    v = tot_ref[0:1, :] * (AUX_WEIGHT * n_dev / (float(total_tok) * total_tok))
    acc[...] = gwr[...]
    red[...] = jnp.zeros_like(red)

    def block(b, _):
        at = pl.ds(pl.multiple_of(b * tb, tb), tb)
        x = x_ref[at, :]
        lane = lax.broadcasted_iota(jnp.int32, (tb, LANES), 1)
        p, lz = router_rows(x, wr, lane, n_dev)
        dl = base_grad(p, lz, v, 2.0 * Z_WEIGHT / total_tok)
        dl2, dl3 = split_rows(dl)
        gx_ref[at, :] = dot(dl3, wrt[...]).astype(BF)
        drop = (slot[pl.ds(b, 1), :] >= n_dev * cap).astype(F32)
        drop = jnp.broadcast_to(drop, (LANES, LANES)).T.astype(BF)
        gw = dot(x.T, dl2 * jnp.concatenate([drop, drop], axis=1))
        acc[...] += gw[:, :LANES] + gw[:, LANES:]
        red[0:1, :] += jnp.sum(p, axis=0, keepdims=True)
        red[1:2, :] += jnp.sum(jnp.broadcast_to(lz * lz, (tb, LANES)), axis=0, keepdims=True)
        return 0
    lax.fori_loop(0, t // tb, block, 0)

    gt = acc[...].T
    part[...] = jnp.zeros_like(part)
    for k in range(nk):
        part[pl.ds(k, n_dev, stride=8), :] = gt[0:n_dev, k * LANES:(k + 1) * LANES]
    for k in (0, 1):
        part[pl.ds(nk + k, n_dev, stride=8), :] = jnp.broadcast_to(red[k:k + 1, :], (n_dev, LANES))

    def tile(ref, i):
        return ref.at[pl.ds(pl.multiple_of(i * 8, 8), 8)]

    def rs_copy(k, slot):
        peer = lax.rem(me + k, n_dev)
        at = me if slot else peer
        return pltpu.make_async_remote_copy(
            src_ref=tile(part, peer), dst_ref=tile(fin, n_dev + at), send_sem=rs_send.at[peer],
            recv_sem=rs_recv.at[at], device_id=(peer,), device_id_type=MESH_ID)

    def ag_copy(k, slot):
        peer = lax.rem(me + k, n_dev)
        at = me if slot else peer
        return pltpu.make_async_remote_copy(
            src_ref=red, dst_ref=tile(fin, at), send_sem=ag_send.at[peer],
            recv_sem=ag_recv.at[at], device_id=(peer,), device_id_type=MESH_ID)

    def others(fn):
        def body(k, _):
            fn(k)
            return 0
        lax.fori_loop(1, n_dev, body, 0)
    others(lambda k: rs_copy(k, True).start())
    grad_copy(1).start()
    for c in own:
        c.wait()
    put(bo, 0, rank)
    put(bm, hd, rank)
    big[n_dev * cap] = jnp.ones((SLAB, LANES), F32)
    each(wait)

    def combine(b, _):
        def fetch(q, _):
            rows = [big[slot_sm[b, q * UNROLL + u]] for u in range(UNROLL)]
            tmp[pl.ds(pl.multiple_of(q * (SLAB * UNROLL), 8), SLAB * UNROLL), :] = jnp.concatenate(rows, axis=0)
            return 0
        lax.fori_loop(0, LANES // UNROLL, fetch, 0)
        at = pl.ds(pl.multiple_of(b * LANES, LANES), LANES)
        drop = tmp[pl.ds(nk, LANES, stride=SLAB), :] > 0.5
        for k in range(nk):
            lanes = slice(k * LANES, (k + 1) * LANES)
            got = tmp[pl.ds(k, LANES, stride=SLAB), :]
            gx_ref[at, lanes] = jnp.where(drop, gx_ref[at, lanes].astype(F32), got).astype(BF)
        return 0
    lax.fori_loop(0, t // LANES, combine, 0)
    mine = pl.ds(pl.multiple_of(me * 8, 8), 8)
    red[...] = part[mine, :]

    def collect(k):
        rs_copy(k, False).wait_recv()
        src = lax.rem(me + k, n_dev)
        red[...] += fin[pl.ds(pl.multiple_of((n_dev + src) * 8, 8), 8), :]
    others(collect)
    others(lambda k: ag_copy(k, True).start())
    fin[mine, :] = red[...]
    others(lambda k: ag_copy(k, False).wait_recv())
    others(lambda k: rs_copy(k, False).wait_send())
    others(lambda k: ag_copy(k, False).wait_send())
    each(drain)
    for a in (0, 1):
        grad_copy(a).wait()


def finish_call(slot, gx, gwi, gwo, x, tot, wr, wrt, gwr, total_tok):
    n_dev, cap, d = gx.shape
    hd = n_dev // 2
    dma = pltpu.SemaphoreType.DMA
    sd = jax.ShapeDtypeStruct
    rows = pltpu.VMEM((hd, cap, d), BF)
    return pl.pallas_call(
        functools.partial(finish_kernel, (hd, n_dev, cap, LANES, total_tok)),
        out_shape=[sd(x.shape, BF), sd(gwi.shape, F32), sd(gwo.shape, F32), sd((2 * n_dev * 8, LANES), F32)],
        in_specs=[SM] + [HBM] * 3 + [VM] * 6, out_specs=[VM, HBM, HBM, VM],
        scratch_shapes=[rows, rows, pltpu.VMEM((n_dev * cap + 1, SLAB, LANES), F32), pltpu.VMEM((LANES * SLAB, LANES), F32),
                        pltpu.VMEM((d, LANES), F32), pltpu.VMEM((n_dev * 8, LANES), F32), pltpu.VMEM((8, LANES), F32),
                        dma((2,)), dma((2, hd)), dma((2, hd))] + [dma((n_dev,))] * 4 + [dma((2,))] * 2, name='finish',
        cost_estimate=pl.CostEstimate(flops=10 ** 10, bytes_accessed=32 * 2 ** 20, transcendentals=0),
        compiler_params=pltpu.CompilerParams(has_side_effects=True, vmem_limit_bytes=VMEM_LIMIT))(
            slot, gx, gwi, gwo, x, slot, tot, wr, wrt, gwr)


def route_kernel(ne, cap, half_ref, idx_ref, slot_ref, cnt_ref, hot, cum):
    nb = idx_ref.shape[0]
    expert = lax.broadcasted_iota(jnp.int32, (ne, LANES), 0)
    shift = half_ref[0] * (ne // 2)
    for b in range(nb):
        hot[b * ne:(b + 1) * ne, :] = (expert == idx_ref[b:b + 1, :]).astype(F32)
    r = lax.broadcasted_iota(jnp.int32, (LANES, 2 * LANES), 0)
    c = lax.broadcasted_iota(jnp.int32, (LANES, 2 * LANES), 1)
    tri = ((r <= c) | (c >= LANES)).astype(F32).astype(BF)
    cum[...] = dot(hot[...].astype(BF), tri)
    carry = jnp.zeros((ne, LANES), F32)
    for b in range(nb):
        block = cum[b * ne:(b + 1) * ne, :]
        pos = jnp.sum(hot[b * ne:(b + 1) * ne, :] * (block[:, :LANES] + carry), axis=0, keepdims=True) - 1.0
        pos = pos.astype(jnp.int32)
        rel = idx_ref[b:b + 1, :] + shift
        rel = jnp.where(rel >= ne, rel - ne, rel)
        slot_ref[b:b + 1, :] = jnp.where(pos < cap, rel * cap + pos, ne * cap)
        carry = carry + block[:, LANES:]
    full = jnp.concatenate([carry, jnp.zeros((LANES - ne, LANES), F32)], axis=0)
    cnt_ref[...] = full.T[0:8, :]


def route_call(half, idx, ne, cap):
    nb = idx.shape[0] // LANES
    sd = jax.ShapeDtypeStruct
    return pl.pallas_call(
        functools.partial(route_kernel, ne, cap), out_shape=[sd((nb, LANES), jnp.int32), sd((8, LANES), F32)],
        in_specs=[SM, VM], out_specs=[VM, VM],
        scratch_shapes=[pltpu.VMEM((nb * ne, LANES), F32), pltpu.VMEM((nb * ne, 2 * LANES), F32)], name='route',
        compiler_params=pltpu.CompilerParams(vmem_limit_bytes=VMEM_LIMIT))(half, idx.reshape(nb, LANES))


def dispatch_kernel(nb, tb, ne, cap, d, slot_ref, cnt_ref, x_ref, dy_ref, sx_ref, sdy_ref, tmp, big):
    i = pl.program_id(0)
    nk = d // LANES

    @pl.when(i < nb)
    def _():
        xf = x_ref[...].astype(F32)
        df = dy_ref[...].astype(F32)
        for k in range(nk):
            tmp[pl.ds(k, tb, stride=8), :] = xf[:, k * LANES:(k + 1) * LANES]
            tmp[pl.ds(4 + k, tb, stride=8), :] = df[:, k * LANES:(k + 1) * LANES]

        def place(q, _):
            row = i * (tb // LANES) + q // (LANES // UNROLL)
            col = lax.rem(q, LANES // UNROLL) * UNROLL
            at = [slot_ref[row, col + u] * 8 for u in range(UNROLL)]
            rows = tmp[pl.ds(pl.multiple_of(q * (8 * UNROLL), 8), 8 * UNROLL), :]
            for u in range(UNROLL):
                big[pl.ds(pl.multiple_of(at[u], 8), 8), :] = rows[8 * u:8 * u + 8]
            return 0
        lax.fori_loop(0, tb // UNROLL, place, 0)

    @pl.when(i >= nb)
    def _():
        e = i - nb
        n = cnt_ref[e]
        ok = lax.broadcasted_iota(jnp.int32, (cap, LANES), 0) < n
        base = e * (cap * 8)
        for k in range(nk):
            xk = big[pl.ds(base + k, cap, stride=8), :]
            sx_ref[0, :, k * LANES:(k + 1) * LANES] = jnp.where(ok, xk, 0.0).astype(BF)
            dk = big[pl.ds(base + 4 + k, cap, stride=8), :]
            sdy_ref[0, :, k * LANES:(k + 1) * LANES] = jnp.where(ok, dk, 0.0).astype(BF)


def dispatch_call(slot, cnt, x, dy, ne, cap):
    t, d = x.shape
    tb = 512
    nb = t // tb
    sd = jax.ShapeDtypeStruct((ne, cap, d), BF)
    tok = pl.BlockSpec((tb, d), lambda i: (jnp.minimum(i, nb - 1), 0))
    out = pl.BlockSpec((1, cap, d), lambda i: (jnp.maximum(i - nb, 0), 0, 0))
    return pl.pallas_call(
        functools.partial(dispatch_kernel, nb, tb, ne, cap, d), grid=(nb + ne,), out_shape=[sd, sd],
        in_specs=[SM, SM, tok, tok], out_specs=[out, out],
        scratch_shapes=[pltpu.VMEM((tb * 8, LANES), F32), pltpu.VMEM((ne * cap * 8 + 8, LANES), F32)], name='dispatch',
        compiler_params=pltpu.CompilerParams(vmem_limit_bytes=VMEM_LIMIT))(slot, cnt, x, dy)


def split_router(w_router):
    d, ne = w_router.shape
    hi = lax.reduce_precision(w_router, 8, 7)
    lo = lax.reduce_precision(w_router - hi, 8, 7)
    pad = lambda a: jnp.pad(a, ((0, 0), (0, LANES - ne)))
    wr = jnp.concatenate([pad(hi), pad(lo)], axis=1).astype(BF)
    wrt = jnp.concatenate([pad(hi), pad(hi), pad(lo)], axis=1).T.astype(BF)
    return wr, wrt


def solution(mesh):
    n_dev = mesh.shape['ep']
    hd = n_dev // 2
    mirror = [(i, (i + hd) % n_dev) for i in range(n_dev)]

    def expert_layer(x_tokens, w_router, expert_idx, w_in, w_out, grad_y):
        tokens, d_model = x_tokens.shape
        ff = w_in.shape[-1]
        ne = n_dev
        capacity = (5 * tokens + 4 * ne - 1) // (4 * ne)
        total_tok = tokens * n_dev
        me = lax.axis_index('ep')
        half = me // hd
        w_in_o, w_out_o = w_in[0], w_out[0]
        w_in_m = lax.ppermute(w_in_o, 'ep', mirror)
        wr, wrt = split_router(w_router)

        slot, cnt = route_call(half.reshape(1).astype(jnp.int32), expert_idx, ne, capacity)
        own = cnt[0, :ne].astype(jnp.int32)
        rel_cnt = jnp.where(half == 0, own, jnp.roll(own, hd))
        sx, sdy = dispatch_call(slot, rel_cnt, x_tokens, grad_y, ne, capacity)
        gx, gwi_o, gwo_o, gwi_m, gwo_m, gwr, tot = expert_call(
            (n_dev, hd, capacity, d_model, ff, 512, total_tok), cnt, sx, sdy, w_in_o, w_out_o, w_in_m, wr, wrt)
        grad_x, gwi_r, gwo_r, fin = finish_call(slot, gx, gwi_m, gwo_m, x_tokens, tot, wr, wrt, gwr, total_tok)
        fin = fin[:ne * 8].reshape(ne, 8, LANES)
        nk = d_model // LANES
        grad_w_router = fin[:, :nk].reshape(ne, d_model).T
        aux_loss = AUX_WEIGHT * ne * jnp.sum(tot[0, :ne] / total_tok * fin[0, nk, :ne] / total_tok)
        z_loss = Z_WEIGHT * fin[0, nk + 1, 0] / total_tok
        return grad_x, (gwi_o + gwi_r)[None], (gwo_o + gwo_r)[None], grad_w_router, aux_loss, z_loss

    return jax.shard_map(expert_layer, mesh=mesh,
                         in_specs=(P('ep', None), P(None, None), P('ep'), P('ep', None, None), P('ep', None, None), P('ep', None)),
                         out_specs=(P('ep', None), P('ep', None, None), P('ep', None, None), P(None, None), P(), P()),
                         check_vma=False)
```

time: 605 us -> 559 us (0.924)
  Pallas kernels: 576 us -> 530 us
    pallas_call x4 -> x2, Pallas kernels: 526 us -> 480 us  [the longest x1 250 us: expert_call(): pl.pallas_call(functools.partial(expert_kernel, cfg), out_shape=[sd((n_de...]
  transfers between devices with their start and end apart: 4 -> 1, of which waited for: 0 -> 0; matrix products, arithmetic and copies ran while one was open for 2% -> 1% of each run, Pallas kernels for 78% -> 9%
where the time goes in v5:
time: 559 us; the launch traced here: 558 us
  Pallas kernels  530 us (95%)
  local copies, waits for them, and re-layouts  10.1 us (2%)
  other arithmetic  10 us (2%)
    pallas_call x1, Pallas kernels, expert_call(): pl.pallas_call(functools.partial(expert_kernel, cfg), out_shape=[sd((n_de...  250 us
    pallas_call x1, Pallas kernels, finish_call(): pl.pallas_call(functools.partial(finish_kernel, (hd, n_dev, cap, LANES, t...  230 us
    pallas_call x1, Pallas kernels, dispatch_call(): pl.pallas_call(functools.partial(dispatch_kernel, nb, tb, ne, cap, d), gr...  47.7 us
  transfers between devices with their start and end apart: 1, of which 0 were waited for; matrix products, arithmetic and copies ran while one was open for 1% of the time, Pallas kernels for 9%

profile of v5, /device:TPU:0, one launch (start us, length us, event | category | flops | bytes accessed | tf_op | source)
XLA Modules:
  0.0 558.4 jit_solution(12747785758286815113)
XLA Ops:
  0.6 4.2 collective-permute-start
  4.8 0.8 fusion.3
  5.7 0.8 copy.14.refs_6_.wr
  6.5 2.0 route.1
  8.5 0.7 slice_convert_fusion
  9.1 0.1 slice_bitcast_fusion.3
  9.2 1.3 broadcast_select_fusion.cnt_ref
  10.5 47.7 %dispatch.1 = (bf16[32,320,384]{2,1,0:T(8,128)(2,1)}, bf16[32,320,384]{2,1,0:T(8,128)(2,1)}) custom-call(s32[64,128]{1,0:T(8,128)} %get-tuple-element.21.slot_ref.slot_sm.slot, s32[32]{0:T(128)} %broadcast_select_fusion.cnt_ref, bf16[8192,384]{1,0:T(8,128)(2,1)} %x_ref.3, bf16[8192,384]{1,0:T(8,128)(2,1)} %dy_ref.1), custom_call_target="tpu_custom_call" | custom-call | tf_op jit(solution)/shard_map/dispatch/pallas_call | solution.py:481
  58.2 0.7 maximum_bitcast_fusion.refs_7_.wrt
  58.9 0.0 collective-permute-done.refs_5_
  58.9 1.0 copy-done.3
  60.0 250.2 %experts.1 = (bf16[32,320,384]{2,1,0:T(8,128)(2,1)}, f32[384,1536]{1,0:T(8,128)}, f32[1536,384]{1,0:T(8,128)}, f32[384,1536]{1,0:T(8,128)}, f32[1536,384]{1,0:T(...) custom-call(f32[8,128]{1,0:T(8,128)} %get-tuple-element.22.refs_0_, bf16[32,320,384]{2,1,0:T(8,128)(2,1)} %get-tuple-element.23.refs_1_, ...), custom_call_target="tpu_custom_call" | custom-call | flops 72477573120 | bytes 67108864 | tf_op jit(solution)/shard_map/experts/pallas_call | solution.py:227
  310.2 0.0 copy-start.1
  310.2 229.9 %finish.1 = (bf16[8192,384]{1,0:T(8,128)(2,1)}, f32[384,1536]{1,0:T(8,128)}, f32[1536,384]{1,0:T(8,128)}, f32[512,128]{1,0:T(8,128)}) custom-call(s32[64,128]{1,0:T(8,128)} %get-tuple-element.21.slot_ref.slot_sm.slot, bf16[32,320,384]{2,1,0:T(8,128)(2,1)} %get-tuple-element.25.rows, f32[384,1536]{1,0:T(8,128)} %get-tuple-element.26.gwi, ...), custom_call_target="tpu_custom_call" | custom-call | flops 10000000000 | bytes 33554432 | tf_op jit(solution)/shard_map/finish/pallas_call | solution.py:394
  540.2 0.9 slice_bitcast_fusion
  541.1 0.5 slice.44
  541.6 1.3 fusion.2
  542.9 0.6 copy.18
  543.5 0.0 copy-done.1
  543.5 3.5 add_bitcast_fusion
  547.0 0.0 copy-done
  547.0 0.0 copy-done.2
  547.0 1.8 add_bitcast_fusion.1
  550.0 6.1 %copy.20 = bf16[8192,384]{1,0:T(8,128)(2,1)} copy(bf16[8192,384]{1,0:T(8,128)(2,1)} %get-tuple-element.48) | data formatting | bytes 12582912
  (6 shorter events, 0.1 us)
Async XLA Ops:
  0.6 58.3 %collective-permute-start = (bf16[384,1536]{1,0:T(8,128)(2,1)}, bf16[384,1536]{1,0:T(8,128)(2,1)S(1)}, u32[]{:S(2)}, u32[]{:S(2)}) collective-permute-start(bf16[384,1536]{1,0:T(8,128)(2,1)} %bitcast.41), channel_id=1, source_target_pairs={{0,16},{1,17},{2,18},{3,19},{4,20},{5,21},{6,22},{7,23},{8,24},{9,... | collective-permute-start | bytes 3538952 | tf_op jit(solution)/shard_map/ppermute | solution.py:512
  58.9 1.0 copy-start.3
  310.2 233.3 %copy-start.1 = (f32[1536,384]{1,0:T(8,128)S(1)}, f32[1536,384]{1,0:T(8,128)}, u32[]{:S(2)}) copy-start(f32[1536,384]{1,0:T(8,128)} %get-tuple-element.33) | copy-start | bytes 7077892
  543.5 3.5 copy-start
  543.5 3.5 copy-start.2

commit v6 on v5

--- a/solution.py
+++ b/solution.py
@@ -99,8 +99,8 @@
             token_copy(part, 0, peer, rank).start()
             token_copy(part, 1, peer, rank).start()
         each(one)
+    weight.start()
     start(0)
-    weight.start()
     start(1)
 
     gwr[...] = jnp.zeros_like(gwr)
@@ -233,7 +233,7 @@
 
 
 def finish_kernel(cfg, slot_sm, rows, gwi, gwo, x_ref, slot, tot_ref, wr, wrt, gwr, gx_ref, gwi_r, gwo_r, fin,
-                  bo, bm, big, tmp, acc, part, red, loc_sem, send_sem, recv_sem, rs_send, rs_recv, ag_send, ag_recv,
+                  x_buf, x_sem, bo, bm, big, tmp, acc, part, red, loc_sem, send_sem, recv_sem, rs_send, rs_recv, ag_send, ag_recv,
                   gr_send, gr_recv):
     hd, n_dev, cap, tb, total_tok = cfg
     me = lax.axis_index('ep')
@@ -291,16 +291,19 @@
         lax.fori_loop(1, hd // 2, body, 0)
     each(start)
     grad_copy(0).start()
+    fetch_x = pltpu.make_async_copy(x_ref, x_buf, x_sem)
+    fetch_x.start()
     for c in own:
         c.start()
 
     v = tot_ref[0:1, :] * (AUX_WEIGHT * n_dev / (float(total_tok) * total_tok))
     acc[...] = gwr[...]
     red[...] = jnp.zeros_like(red)
+    fetch_x.wait()
 
     def block(b, _):
         at = pl.ds(pl.multiple_of(b * tb, tb), tb)
-        x = x_ref[at, :]
+        x = x_buf[at, :]
         lane = lax.broadcasted_iota(jnp.int32, (tb, LANES), 1)
         p, lz = router_rows(x, wr, lane, n_dev)
         dl = base_grad(p, lz, v, 2.0 * Z_WEIGHT / total_tok)
@@ -394,8 +397,8 @@
     return pl.pallas_call(
         functools.partial(finish_kernel, (hd, n_dev, cap, LANES, total_tok)),
         out_shape=[sd(x.shape, BF), sd(gwi.shape, F32), sd(gwo.shape, F32), sd((2 * n_dev * 8, LANES), F32)],
-        in_specs=[SM] + [HBM] * 3 + [VM] * 6, out_specs=[VM, HBM, HBM, VM],
-        scratch_shapes=[rows, rows, pltpu.VMEM((n_dev * cap + 1, SLAB, LANES), F32), pltpu.VMEM((LANES * SLAB, LANES), F32),
+        in_specs=[SM] + [HBM] * 4 + [VM] * 5, out_specs=[VM, HBM, HBM, VM],
+        scratch_shapes=[pltpu.VMEM(x.shape, BF), dma, rows, rows, pltpu.VMEM((n_dev * cap + 1, SLAB, LANES), F32), pltpu.VMEM((LANES * SLAB, LANES), F32),
                         pltpu.VMEM((d, LANES), F32), pltpu.VMEM((n_dev * 8, LANES), F32), pltpu.VMEM((8, LANES), F32),
                         dma((2,)), dma((2, hd)), dma((2, hd))] + [dma((n_dev,))] * 4 + [dma((2,))] * 2, name='finish',
         cost_estimate=pl.CostEstimate(flops=10 ** 10, bytes_accessed=32 * 2 ** 20, transcendentals=0),
@@ -460,26 +463,26 @@
 
     @pl.when(i >= nb)
     def _():
-        e = i - nb
-        n = cnt_ref[e]
-        ok = lax.broadcasted_iota(jnp.int32, (cap, LANES), 0) < n
-        base = e * (cap * 8)
-        for k in range(nk):
-            xk = big[pl.ds(base + k, cap, stride=8), :]
-            sx_ref[0, :, k * LANES:(k + 1) * LANES] = jnp.where(ok, xk, 0.0).astype(BF)
-            dk = big[pl.ds(base + 4 + k, cap, stride=8), :]
-            sdy_ref[0, :, k * LANES:(k + 1) * LANES] = jnp.where(ok, dk, 0.0).astype(BF)
+        for q in (0, 1):
+            e = 2 * (i - nb) + q
+            ok = lax.broadcasted_iota(jnp.int32, (cap, LANES), 0) < cnt_ref[e]
+            base = e * (cap * 8)
+            for k in range(nk):
+                xk = big[pl.ds(base + k, cap, stride=8), :]
+                sx_ref[q, :, k * LANES:(k + 1) * LANES] = jnp.where(ok, xk, 0.0).astype(BF)
+                dk = big[pl.ds(base + 4 + k, cap, stride=8), :]
+                sdy_ref[q, :, k * LANES:(k + 1) * LANES] = jnp.where(ok, dk, 0.0).astype(BF)
 
 
 def dispatch_call(slot, cnt, x, dy, ne, cap):
     t, d = x.shape
-    tb = 512
+    tb = 1024
     nb = t // tb
     sd = jax.ShapeDtypeStruct((ne, cap, d), BF)
     tok = pl.BlockSpec((tb, d), lambda i: (jnp.minimum(i, nb - 1), 0))
-    out = pl.BlockSpec((1, cap, d), lambda i: (jnp.maximum(i - nb, 0), 0, 0))
+    out = pl.BlockSpec((2, cap, d), lambda i: (jnp.maximum(i - nb, 0), 0, 0))
     return pl.pallas_call(
-        functools.partial(dispatch_kernel, nb, tb, ne, cap, d), grid=(nb + ne,), out_shape=[sd, sd],
+        functools.partial(dispatch_kernel, nb, tb, ne, cap, d), grid=(nb + ne // 2,), out_shape=[sd, sd],
         in_specs=[SM, SM, tok, tok], out_specs=[out, out],
         scratch_shapes=[pltpu.VMEM((tb * 8, LANES), F32), pltpu.VMEM((ne * cap * 8 + 8, LANES), F32)], name='dispatch',
         compiler_params=pltpu.CompilerParams(vmem_limit_bytes=VMEM_LIMIT))(slot, cnt, x, dy)

time: 559 us -> 554 us (level)
  Pallas kernels: 530 us -> 523 us
    pallas_call x1, Pallas kernels: 250 us -> 245 us  [expert_call(): pl.pallas_call(functools.partial(expert_kernel, cfg), out_shape=[sd((n_de...]
  transfers between devices with their start and end apart: 1 -> 1, of which waited for: 0 -> 1; matrix products, arithmetic and copies ran while one was open for 1% -> 1% of each run, Pallas kernels for 9% -> 8%
where the time goes in v6:
time: 554 us
  Pallas kernels  523 us (94%)
  local copies, waits for them, and re-layouts  10.1 us (2%)
  other arithmetic  10 us (2%)
    pallas_call x1, Pallas kernels, expert_call(): pl.pallas_call(functools.partial(expert_kernel, cfg), out_shape=[sd((n_de...  245 us
    pallas_call x1, Pallas kernels, finish_call(): pl.pallas_call(functools.partial(finish_kernel, (hd, n_dev, cap, LANES, t...  234 us
    pallas_call x1, Pallas kernels, dispatch_call(): pl.pallas_call(functools.partial(dispatch_kernel, nb, tb, ne, cap, d), gr...  42.6 us
  transfers between devices with their start and end apart: 1, of which 1 were waited for; matrix products, arithmetic and copies ran while one was open for 1% of the time, Pallas kernels for 8%

profile of v6, /device:TPU:0, one launch (start us, length us, event | category | flops | bytes accessed | tf_op | source)
XLA Modules:
  0.0 553.8 jit_solution(11004461539838867964)
XLA Ops:
  0.6 4.2 collective-permute-start
  4.8 0.8 fusion.3
  5.7 0.8 copy.14.refs_6_.wr
  6.5 2.0 route.1
  8.5 0.7 slice_convert_fusion
  9.1 0.1 slice_bitcast_fusion.3
  9.2 1.3 broadcast_select_fusion.cnt_ref
  10.5 42.6 %dispatch.1 = (bf16[32,320,384]{2,1,0:T(8,128)(2,1)}, bf16[32,320,384]{2,1,0:T(8,128)(2,1)}) custom-call(s32[64,128]{1,0:T(8,128)} %get-tuple-element.21.slot_ref.slot_sm.slot, s32[32]{0:T(128)} %broadcast_select_fusion.cnt_ref, bf16[8192,384]{1,0:T(8,128)(2,1)} %x_ref.3, bf16[8192,384]{1,0:T(8,128)(2,1)} %dy_ref.1), custom_call_target="tpu_custom_call" | custom-call | tf_op jit(solution)/shard_map/dispatch/pallas_call | solution.py:484
  53.1 0.7 maximum_bitcast_fusion.refs_7_.wrt
  53.8 2.1 collective-permute-done.refs_5_
  56.0 1.0 copy-done.3
  57.0 244.6 %experts.1 = (bf16[32,320,384]{2,1,0:T(8,128)(2,1)}, f32[384,1536]{1,0:T(8,128)}, f32[1536,384]{1,0:T(8,128)}, f32[384,1536]{1,0:T(8,128)}, f32[1536,384]{1,0:T(...) custom-call(f32[8,128]{1,0:T(8,128)} %get-tuple-element.22.refs_0_, bf16[32,320,384]{2,1,0:T(8,128)(2,1)} %get-tuple-element.23.refs_1_, ...), custom_call_target="tpu_custom_call" | custom-call | flops 72477573120 | bytes 67108864 | tf_op jit(solution)/shard_map/experts/pallas_call | solution.py:227
  301.6 0.0 copy-start.1
  301.6 234.0 %finish.1 = (bf16[8192,384]{1,0:T(8,128)(2,1)}, f32[384,1536]{1,0:T(8,128)}, f32[1536,384]{1,0:T(8,128)}, f32[512,128]{1,0:T(8,128)}) custom-call(s32[64,128]{1,0:T(8,128)} %get-tuple-element.21.slot_ref.slot_sm.slot, bf16[32,320,384]{2,1,0:T(8,128)(2,1)} %get-tuple-element.25.rows, f32[384,1536]{1,0:T(8,128)} %get-tuple-element.26.gwi, ...), custom_call_target="tpu_custom_call" | custom-call | flops 10000000000 | bytes 33554432 | tf_op jit(solution)/shard_map/finish/pallas_call | solution.py:397
  535.6 0.9 slice_bitcast_fusion
  536.5 0.5 slice.44
  537.0 1.3 fusion.2
  538.3 0.6 copy.18
  538.9 0.0 copy-done.1
  538.9 3.5 add_bitcast_fusion
  542.4 0.0 copy-done
  542.4 0.0 copy-done.2
  542.4 1.8 add_bitcast_fusion.1
  545.5 6.1 %copy.20 = bf16[8192,384]{1,0:T(8,128)(2,1)} copy(bf16[8192,384]{1,0:T(8,128)(2,1)} %get-tuple-element.48) | data formatting | bytes 12582912
  (6 shorter events, 0.1 us)
Async XLA Ops:
  0.6 55.3 %collective-permute-start = (bf16[384,1536]{1,0:T(8,128)(2,1)}, bf16[384,1536]{1,0:T(8,128)(2,1)S(1)}, u32[]{:S(2)}, u32[]{:S(2)}) collective-permute-start(bf16[384,1536]{1,0:T(8,128)(2,1)} %bitcast.41), channel_id=1, source_target_pairs={{0,16},{1,17},{2,18},{3,19},{4,20},{5,21},{6,22},{7,23},{8,24},{9,... | collective-permute-start | bytes 3538952 | tf_op jit(solution)/shard_map/ppermute | solution.py:515
  56.0 1.0 copy-start.3
  301.6 237.3 %copy-start.1 = (f32[1536,384]{1,0:T(8,128)S(1)}, f32[1536,384]{1,0:T(8,128)}, u32[]{:S(2)}) copy-start(f32[1536,384]{1,0:T(8,128)} %get-tuple-element.33) | copy-start | bytes 7077892
  538.9 3.5 copy-start
  538.9 3.5 copy-start.2
